TPU v7x, 32 devices: a whole 2x2x4 slice. The times are simulated.
32 devices in a mesh: row: 8 (over z, core), col: 4 (over y, x).
Axes of the slice: x: 2, y: 2, z: 4, core: 2. Of those that a mesh axis runs over, the one named last changes fastest.
Arguments:
- factor: bfloat16 [8192, 8192], P('row', 'col'), as said below
- sel_tiles: int32 [32], replicated, may hold values from 0 to 63, as said below
- coupling: bfloat16 [8192, 2048], P('col', 'row')
Outputs:
- root_inverse: float32 [8192, 8192], P('row', 'col')
- child_inverse: float32 [2048, 8192], P('col', 'row')
Inputs may be any that keep to these rules, and one draw needn't show every extreme that they name: sel_tiles holds 32 distinct tile indices in increasing order; rows of coupling outside the listed tiles are zero. factor is lower triangular with a diagonal between 1 and 1.5.
All inputs are finite; a program needn't handle non-finite values.
Results may differ from a plain program's by a relative error of at most 0.003.
Values may be sent and summed in bfloat16 or wider, within the bound.
A program may use at most 128 MiB of HBM per device.

v0:
```python
import functools
import math

import jax
import jax.numpy as jnp
from jax import lax
from jax.experimental import pallas as pl
from jax.experimental.pallas import tpu as pltpu
from jax.sharding import PartitionSpec as P

TILE = 128
MESH = pl.DeviceIdType.MESH
SKEW = 2


def gather_kernel(dims, f_ref, a_ref, b_ref, recv_a, recv_b, send_z, send_p, send_b, send_f, local_a, stage):
    levels, wide, high, cores, chunks = dims
    rows, width = f_ref.shape
    narrow = width // cores
    h = rows // chunks
    r, c = lax.axis_index("row"), lax.axis_index("col")
    k, z = lax.rem(r, cores), r // cores
    x, y = lax.rem(c, wide), c // wide
    x0, y0 = lax.rem(z, wide), z // wide
    source = c == z

    def chunk_rows(block, j):
        return pl.ds(pl.multiple_of(block * rows + j * h, h), h)

    def remote(src, dst, send, recv, row, col):
        return pltpu.make_async_remote_copy(
            src_ref=src, dst_ref=dst, send_sem=send, recv_sem=recv,
            device_id=(row, col), device_id_type=MESH,
        )

    def copies(t, j):
        m = z + t
        inside = m < levels
        has = inside & (m >= c)
        block = m * cores + k
        at = chunk_rows(block, j)
        if t == 0:
            def src(cols):
                return f_ref.at[pl.ds(j * h, h), cols]
        else:
            def src(cols):
                return a_ref.at[at, cols]
        everything = pl.ds(0, width)
        found = []
        for kk in range(cores):
            piece = src(pl.ds(kk * narrow, narrow))
            into = b_ref.at[at, :]
            for dx in range(1, wide):
                xt = lax.rem(x + dx, wide)
                found.append((
                    source & inside & (m >= y * wide + xt),
                    remote(piece, into, send_b.at[kk, dx, t, j], recv_b.at[block, j],
                           z * cores + kk, y * wide + xt),
                    False,
                ))
            for dy in range(1, high):
                yt = lax.rem(y + dy, high)
                found.append((
                    source & inside & (m >= yt * wide),
                    remote(piece, into, send_b.at[kk, wide - 1 + dy, t, j], recv_b.at[block, j],
                           z * cores + kk, yt * wide + x),
                    False,
                ))
        found.append((
            has & (z > 0),
            remote(src(everything), a_ref.at[at, :], send_z.at[t, j], recv_a.at[block, j],
                   r - cores, c),
            False,
        ))
        for dk in range(1, cores):
            other = z * cores + lax.rem(k + dk, cores)
            found.append((
                has,
                remote(src(everything), a_ref.at[at, :], send_p.at[dk, t, j], recv_a.at[block, j], other, c),
                False,
            ))
        for kk in range(cores):
            piece = src(pl.ds(kk * narrow, narrow))
            into = b_ref.at[at, :]
            found.append((
                source & inside & (k != kk),
                remote(piece, into, send_b.at[kk, 0, t, j], recv_b.at[block, j], z * cores + kk, c),
                False,
            ))
        return found

    def keep(t, j):
        m = z + t
        at = chunk_rows(m * cores + k, j)
        here = f_ref.at[pl.ds(j * h, h), :] if t == 0 else a_ref.at[at, :]
        inside = (m < levels) & (m >= c)

        @pl.when(inside if t == 0 else inside & source)
        def _():
            load = pltpu.make_async_copy(here, stage, local_a.at[0])
            load.start()
            load.wait()
            if t == 0:
                pltpu.make_async_copy(stage, a_ref.at[at, :], local_a.at[1]).start()
            for kk in range(cores):
                @pl.when(source & (k == kk))
                def _():
                    store = pltpu.make_async_copy(
                        stage.at[:, pl.ds(kk * narrow, narrow)], b_ref.at[at, :], local_a.at[2]
                    )
                    store.start()
                    store.wait()
            if t == 0:
                pltpu.make_async_copy(stage, a_ref.at[at, :], local_a.at[1]).wait()

    def forwards(t, j, p):
        m = z + t
        block = m * cores + p
        part = b_ref.at[chunk_rows(block, j), :]
        mine = (x == x0) & (y != y0) & (m < levels)
        found = []
        for dx in range(1, wide):
            xt = lax.rem(x + dx, wide)
            found.append((
                mine & (m >= y * wide + xt),
                remote(part, part, send_f.at[dx, p, t, j], recv_b.at[block, j], r, y * wide + xt),
            ))
        return mine & (m >= y * wide), found

    def arrived(ref, sem):
        remote(ref, ref, send_z.at[0, 0], sem, r, c).wait_recv()

    def step(t, j):
        m = z + t
        block = m * cores + k
        if t > 0:
            @pl.when((m < levels) & (m >= c))
            def _():
                arrived(a_ref.at[chunk_rows(block, j), :], recv_a.at[block, j])
        for condition, copy, _ in copies(t, j):
            pl.when(condition)(copy.start)
        keep(t, j)

    def forward(t, j):
        for p in range(cores):
            due, found = forwards(t, j, p)
            block = (z + t) * cores + p

            @pl.when(due)
            def _():
                arrived(b_ref.at[chunk_rows(block, j), :], recv_b.at[block, j])
            for condition, copy in found:
                pl.when(condition)(copy.start)

    order = [(t, j) for t in range(levels) for j in range(chunks)]
    for n, (t, j) in enumerate(order):
        step(t, j)
        if n >= SKEW:
            forward(*order[n - SKEW])
    for t, j in order[len(order) - SKEW:]:
        forward(t, j)

    for t, j in order:
        m = z + t
        inside = m < levels
        for dk in range(1, cores):
            block = m * cores + lax.rem(k + dk, cores)

            @pl.when(inside & (m >= c))
            def _():
                arrived(a_ref.at[chunk_rows(block, j), :], recv_a.at[block, j])

            @pl.when(inside & source)
            def _():
                arrived(b_ref.at[chunk_rows(block, j), :], recv_b.at[block, j])
        for p in range(cores):
            block = m * cores + p

            @pl.when(inside & (x != x0) & (m >= c))
            def _():
                arrived(b_ref.at[chunk_rows(block, j), :], recv_b.at[block, j])
        for condition, copy, local in copies(t, j):
            pl.when(condition)(copy.wait if local else copy.wait_send)
        for p in range(cores):
            for condition, copy in forwards(t, j, p)[1]:
                pl.when(condition)(copy.wait_send)


def gather(factor, n_row, n_col):
    rows, width = factor.shape
    cores = n_row // n_col
    wide = next(w for w in range(math.isqrt(n_col), 0, -1) if n_col % w == 0)
    high = n_col // wide
    levels = n_col
    chunks = max(1, 32 // n_row)
    dma = pltpu.SemaphoreType.DMA
    whole = rows * n_row
    return pl.pallas_call(
        functools.partial(gather_kernel, (levels, wide, high, cores, chunks)),
        out_shape=(
            jax.ShapeDtypeStruct((whole, width), factor.dtype),
            jax.ShapeDtypeStruct((whole, width // cores), factor.dtype),
        ),
        in_specs=[pl.BlockSpec(memory_space=pl.ANY)],
        out_specs=(pl.BlockSpec(memory_space=pl.ANY), pl.BlockSpec(memory_space=pl.ANY)),
        scratch_shapes=[
            dma((n_row, chunks)),
            dma((n_row, chunks)),
            dma((levels, chunks)),
            dma((cores, levels, chunks)),
            dma((cores, wide + high, levels, chunks)),
            dma((wide, cores, levels, chunks)),
            dma((3,)),
            pltpu.VMEM((rows // chunks, width), factor.dtype),
        ],
        compiler_params=pltpu.CompilerParams(has_side_effects=True),
        cost_estimate=pl.CostEstimate(flops=0, bytes_accessed=whole * width * 32, transcendentals=0),
    )(factor)


def exchange_kernel(n_col, part_ref, out_ref, send, recv):
    r, c = lax.axis_index("row"), lax.axis_index("col")
    depth = out_ref.shape[1]
    started = []
    for d in range(1, n_col):
        ct = lax.rem(c + d, n_col)
        copy = pltpu.make_async_remote_copy(
            src_ref=part_ref.at[pl.ds(pl.multiple_of(ct * depth, depth), depth), :],
            dst_ref=out_ref.at[d - 1],
            send_sem=send.at[d - 1],
            recv_sem=recv.at[d - 1],
            device_id=(r, ct),
            device_id_type=MESH,
        )
        copy.start()
        started.append(copy)
    for copy in started:
        copy.wait()


def exchange(part, n_col):
    total, width = part.shape
    dma = pltpu.SemaphoreType.DMA
    return pl.pallas_call(
        functools.partial(exchange_kernel, n_col),
        out_shape=jax.ShapeDtypeStruct((n_col - 1, total // n_col, width), part.dtype),
        in_specs=[pl.BlockSpec(memory_space=pl.ANY)],
        out_specs=pl.BlockSpec(memory_space=pl.ANY),
        scratch_shapes=[dma((n_col - 1,)), dma((n_col - 1,))],
        compiler_params=pltpu.CompilerParams(has_side_effects=True),
    )(part)


def body(n_row, n_col, factor, sel_tiles, coupling):
    rows_here = factor.shape[0]
    row_index, col_index = lax.axis_index("row"), lax.axis_index("col")
    cores = n_row // n_col
    below, partner = gather(factor, n_row, n_col)
    coupling_full = lax.all_gather(coupling, "row", axis=1, tiled=True)

    def product(level, below, partner):
        first = level * rows_here * cores
        return lax.dot_general(
            partner[first:], below[first:], (((0,), (0,)), ((), ())), preferred_element_type=jnp.float32
        )

    gram = lax.switch(
        jnp.maximum(row_index // cores, col_index),
        [functools.partial(product, level) for level in range(n_col)],
        below,
        partner,
    )
    rounded = gram.astype(jnp.bfloat16)
    global_rows = row_index * rows_here + jnp.arange(rows_here, dtype=jnp.int32)
    member = jnp.any((global_rows // TILE)[:, None] == sel_tiles[None, :], axis=1)
    part = lax.dot_general(
        coupling_full, rounded, (((0,), (1,)), ((), ())), preferred_element_type=jnp.float32
    ).astype(jnp.bfloat16)
    depth = part.shape[0] // n_col
    arrived = exchange(part, n_col)
    summed = lax.dynamic_slice_in_dim(part, col_index * depth, depth, 0).astype(jnp.float32)
    for d in range(n_col - 1):
        summed = summed + arrived[d].astype(jnp.float32)
    child = jnp.where(member[None, :], -summed, jnp.float32(0.0))
    return (gram, child)


def solution(mesh):
    placed = (P("row", "col"), P(), P("col", "row"))
    return jax.shard_map(
        functools.partial(body, mesh.shape["row"], mesh.shape["col"]),
        mesh=mesh,
        in_specs=placed,
        out_specs=(P("row", "col"), P("col", "row")),
        check_vma=False,
    )
```

profile of v0, /device:TPU:0, one launch (start us, length us, event | category | flops | bytes accessed | tf_op | source)
XLA Modules:
  0.0 499.6 jit_solution(5893461267527661360)
XLA Ops:
  7.2 0.0 all-gather.2.cloned.1.call-start
  7.2 0.7 all-gather.2.cloned.1.call-update
  7.9 372.9 %shard_map.50 = (bf16[8192,2048]{1,0:T(8,128)(2,1)}, bf16[8192,1024]{1,0:T(8,128)(2,1)}) custom-call(bf16[1024,2048]{1,0:T(8,128)(2,1)} %f_ref.1), custom_call_target="tpu_custom_call" | custom-call | bytes 536870912 | tf_op jit(solution)/shard_map/pallas_call | solution.py:198
  380.8 0.0 copy-start
  380.8 44.0 %conditional.1 = (f32[1024,2048]{1,0:T(8,128)}) conditional(s32[]{:T(128)} %clamp.3, (bf16[8192,1024]{1,0:T(8,128)(2,1)}, bf16[8192,2048]{1,0:T(8,128)(2,1)}) %tuple.20, (bf16[8192,1024]{1,0:T(8,128)(2,1)}, bf16[8192,2048]{1,0:T(8,128)(2,1)}) %tuple.20, (bf16[8192,1024]{1,0:T(8,128)(2,1)}, ...), branch_computations={%region_0.1_spmd, %region_1.2_spmd, %region_2.3_spmd, %region_3.4_... | conditional | flops 34359738368 | bytes 58720264 | solution.py:267
  380.8 43.9 %fusion.19 = f32[1024,2048]{1,0:T(8,128)} fusion(bf16[8192,1024]{1,0:T(8,128)(2,1)} %get-tuple-element.18, bf16[8192,2048]{1,0:T(8,128)(2,1)} %get-tuple-element.19), kind=kOutput, calls=%fused_computation.27 | convolution fusion | flops 34359738368 | bytes 58720256 | tf_op jit(solution)/shard_map/cond/branch_0_fun/dot_general | solution.py:263
  424.8 0.0 copy-done
  424.8 0.1 compare_reduce_fusion
  424.9 0.0 all-gather.2.cloned.1.call-done
  424.9 15.1 %fusion.11 = bf16[1024,2048]{0,1:T(8,128)(2,1)} fusion(bf16[2048,2048]{1,0:T(8,128)(2,1)} %all-gather.2.cloned.1.call-done, f32[1024,2048]{1,0:T(8,128)} %get-tuple-element.35), kind=kOutput, calls=%fused_computation.11 | convolution fusion | flops 8594128896 | bytes 20971520 | tf_op jit(solution)/shard_map/dot_general | solution.py:276
  440.0 48.3 %shard_map.51 = bf16[3,512,1024]{2,1,0:T(8,128)(2,1)} custom-call(bf16[2048,1024]{1,0:T(8,128)(2,1)} %bitcast.15), custom_call_target="tpu_custom_call" | custom-call | tf_op jit(solution)/shard_map/pallas_call | solution.py:244
  488.4 4.4 fusion.15
  (1 shorter events, 0.0 us)
Async XLA Ops:
  7.2 417.7 %all-gather.2.cloned.1.call-start = ((), (), s32[]{:S(2)}) async-start(), calls=%async_computation | async-start | bytes 9437184 | tf_op jit(solution)/shard_map/all_gather | solution.py:259
  380.8 44.0 %copy-start = (s32[32]{0:T(128)S(1)}, s32[32]{0:T(128)}, u32[]{:S(2)}) copy-start(s32[32]{0:T(128)} %param.8) | copy-start | bytes 388
Sparse Core Ops, SparseCore 0:
  9.6 142.3 all-gather.1
where the time goes:
time: 500 us
  Pallas kernels  421 us (84%)
  matrix products  59.1 us (12%)
  between operations  14.1 us (3%)
    pallas_call x1, Pallas kernels, gather(): pl.pallas_call(functools.partial(gather_kernel, (levels, wide, high, core...  373 us
    pallas_call x1, Pallas kernels, exchange(): pl.pallas_call(functools.partial(exchange_kernel, n_col), out_shape=jax.S...  48.3 us
    dot_general x1, matrix products, product(): lax.dot_general(partner[first:], below[first:], (((0,), (0,)), ((), ())),...  43.9 us
    dot_general x1, matrix products, body(): lax.dot_general(coupling_full, rounded, (((0,), (1,)), ((), ())), preferr...  15.1 us
  transfers between devices with their start and end apart: 1, of which 0 were waited for; matrix products, arithmetic and copies ran while one was open for 9% of the time, Pallas kernels for 75%

commit v1 on v0

--- a/solution.py
+++ b/solution.py
@@ -218,6 +218,373 @@
     )(factor)
 
 
+LAG = 2
+
+
+def block_flows(pieces):
+    half = pieces // 2
+    found = []
+
+    def add(block, hops, first=0, last=pieces):
+        found.append((block, block, hops, first, last))
+
+    side = [((3, 1), (2, 1)), ((2, 1), (1, 1)), ((1, 1), (1, 3)), ((1, 3), (1, 2)), ((1, 2), (1, 0))]
+    add((3, 3), [((3, 3), (2, 3)), ((2, 3), (1, 3)), ((1, 3), (0, 3)), ((3, 3), (3, 1)), ((3, 3), (3, 2)),
+                 ((3, 2), (3, 0))])
+    add((3, 2), [((3, 2), (2, 2)), ((2, 2), (2, 3)), ((2, 3), (2, 1)), ((2, 2), (2, 0)), ((2, 2), (1, 2)),
+                 ((1, 2), (0, 2))])
+    add((3, 1), side + [((1, 1), (0, 1))], 0, half)
+    add((3, 1), side + [((1, 3), (0, 3)), ((0, 3), (0, 1))], half, pieces)
+    add((3, 0), [((3, 0), (2, 0)), ((2, 0), (2, 1)), ((2, 1), (2, 3)), ((2, 3), (1, 3)), ((1, 3), (0, 3)),
+                 ((0, 3), (0, 1)), ((0, 1), (0, 0)), ((0, 3), (0, 2)), ((2, 0), (1, 0))])
+    add((2, 0), [((2, 0), (1, 0)), ((1, 0), (0, 0)), ((0, 0), (0, 1)), ((0, 0), (0, 2))])
+    add((1, 0), [((1, 0), (0, 0)), ((0, 0), (0, 1))])
+    add((2, 1), [((2, 1), (1, 1)), ((1, 1), (0, 1)), ((1, 1), (1, 0)), ((1, 0), (1, 2))])
+    add((1, 1), [((1, 1), (0, 1)), ((1, 1), (1, 0))])
+    add((2, 2), [((2, 2), (2, 3)), ((2, 3), (2, 1)), ((2, 2), (2, 0)), ((2, 2), (1, 2)), ((1, 2), (0, 2))])
+    return found
+
+
+def coupling_flows(pieces):
+    found = []
+    for c in range(4):
+        for z in range(4):
+            hops = [((a, c), (a - 1, c)) for a in range(z, 0, -1)] + [((a, c), (a + 1, c)) for a in range(z, 3)]
+            found.append((("u", z, c), (z, c), hops, 0, pieces))
+    return found
+
+
+ORDER = [6, 8, 5, 2, 23, 9, 4, 11, 25, 18, 1, 3, 10, 20, 12, 13, 19, 0, 7, 17, 15, 16, 14, 22, 24, 21]
+
+
+@functools.cache
+def plan(pieces, coupling_pieces):
+    flows = block_flows(pieces) + coupling_flows(coupling_pieces)
+    busy, hops = {}, []
+    for index in ORDER:
+        block, source, route, first, last = flows[index]
+        n, at = last - first, {source: 0}
+        for p, q in route:
+            t, used = at[p], busy.setdefault((p, q), [])
+            while any(t < e and s < t + n for s, e in used):
+                t += 1
+            used.append((t, t + n))
+            at[q] = t + LAG
+            hops.append((block, p, q, first, last, t))
+    chips = [(z, c) for z in range(4) for c in range(4)]
+    slots = {chip: {} for chip in chips}
+    needs = {chip: set() for chip in chips}
+    for z, c in chips:
+        for m in range(max(z, c), 4):
+            slots[z, c][m, c] = m
+            needs[z, c].add((m, c))
+            if c != z:
+                slots[z, c][m, z] = 4 + m
+                needs[z, c].add((m, z))
+    for block, p, q, first, last, t in hops:
+        if block[0] != "u" and block not in slots[q]:
+            slots[q][block] = min(set(range(8)) - set(slots[q].values()))
+    due = {}
+    for chip in chips:
+        z, c = chip
+        ready = {(z, c): [1] * pieces}
+        for block, p, q, first, last, t in hops:
+            if q == chip:
+                for j in range(first, last):
+                    ready.setdefault(block, [None] * pieces)[j] = t + LAG + j - first
+        for m in range(max(z, c), 4):
+            both = [ready[m, c], ready[m, z]]
+            due[chip, m] = 1 + max(max(b[2 * j], b[2 * j + 1]) - 2 * j for b in both for j in range(pieces // 2))
+    steps = max([t + last - first + LAG for block, p, q, first, last, t in hops] + [d + pieces for d in due.values()])
+    return hops, slots, needs, due, steps
+
+
+def stream_kernel(pieces, coupling_pieces, f_ref, u_ref, x_ref, ub_ref, g_ref, send, send_u, near, near_u, recv,
+                  recv_u, recv_near, recv_near_u, local, acc, a_buf, b_buf, stage, stage_u, zeros):
+    hops, slots, needs, due, steps = plan(pieces, coupling_pieces)
+    rows, width = f_ref.shape
+    depth, narrow = u_ref.shape
+    h, hu, quarter = rows // pieces, depth // coupling_pieces, width // 4
+    tall = acc.shape[0]
+    r, c = lax.axis_index("row"), lax.axis_index("col")
+    k, z = lax.rem(r, 2), r // 2
+    chip = z * 4 + c
+    owner = z >= c
+
+    def at_rows(slot, core, j):
+        return pl.ds(pl.multiple_of((slot * 2 + core) * rows + j * h, h), h)
+
+    def remote(src, dst, send_sem, recv_sem, row, col):
+        return pltpu.make_async_remote_copy(
+            src_ref=src, dst_ref=dst, send_sem=send_sem, recv_sem=recv_sem,
+            device_id=(row, col), device_id_type=MESH,
+        )
+
+    def shapes(block, j):
+        if block[0] != block[1]:
+            return [(None, width)]
+        part = (k * pieces + j) // (pieces // 2)
+        return [(part == q, (q + 1) * quarter) for q in range(4)]
+
+    def each(block, j, act):
+        if block[0] == "u":
+            act(None)
+            return
+        for condition, columns in shapes(block, j):
+            if condition is None:
+                act(columns)
+            else:
+                pl.when(condition)(functools.partial(act, columns))
+
+    def hop_copy(hop, number, j, columns):
+        block, p, q, first, last, t = hop
+        if block[0] == "u":
+            at = pl.ds(pl.multiple_of(j * hu, hu), hu)
+            src = u_ref.at[at, :] if p == block[1:] else ub_ref.at[block[1] * 2 + k, at, :]
+            return remote(src, ub_ref.at[block[1] * 2 + k, at, :], send_u.at[number, j], recv_u.at[block[1], j],
+                          q[0] * 2 + k, q[1])
+        cols = pl.ds(0, columns)
+        if p == block:
+            src = f_ref.at[pl.ds(pl.multiple_of(j * h, h), h), cols]
+        else:
+            src = x_ref.at[at_rows(slots[p][block], k, j), cols]
+        slot = slots[q][block]
+        return remote(src, x_ref.at[at_rows(slot, k, j), cols], send.at[number, j], recv.at[slot, j],
+                      q[0] * 2 + k, q[1])
+
+    def near_copy(slot, j, src=None):
+        at = at_rows(slot, k, j)
+        return remote(x_ref.at[at, :] if src is None else src, x_ref.at[at, :], near.at[slot, j],
+                      recv_near.at[slot, j], z * 2 + 1 - k, c)
+
+    def near_arrival(slot, j):
+        ref = x_ref.at[at_rows(slot, 1 - k, j), :]
+        return remote(ref, ref, near.at[slot, j], recv_near.at[slot, j], r, c)
+
+    def near_copy_u(level, j, src=None):
+        at = pl.ds(pl.multiple_of(j * hu, hu), hu)
+        ref = ub_ref.at[level * 2 + k, at, :]
+        return remote(ref if src is None else src, ref, near_u.at[level, j], recv_near_u.at[level, j],
+                      z * 2 + 1 - k, c)
+
+    def own_rows(j):
+        return f_ref.at[pl.ds(pl.multiple_of(j * h, h), h), :]
+
+    def own_rows_u(j):
+        return u_ref.at[pl.ds(pl.multiple_of(j * hu, hu), hu), :]
+
+    chips = [(a, b) for a in range(4) for b in range(4)]
+    incoming = {chip_: [hop for hop in hops if hop[2] == chip_] for chip_ in chips}
+    outgoing = {chip_: [] for chip_ in chips}
+    count, count_u = {}, {}
+    for hop in hops:
+        counts = count_u if hop[0][0] == "u" else count
+        number = counts.get(hop[1], 0)
+        counts[hop[1]] = number + 1
+        outgoing[hop[1]].append((hop, number))
+
+    zeros[...] = jnp.zeros_like(zeros)
+
+    def fill(slot, begin):
+        def one(j, carry):
+            for condition, columns in shapes((0, 0), j):
+                if columns < width:
+                    copy = pltpu.make_async_copy(
+                        zeros.at[:, pl.ds(0, width - columns)],
+                        x_ref.at[at_rows(slot, k, j), pl.ds(columns, width - columns)], local.at[1])
+
+                    @pl.when(condition)
+                    def _():
+                        copy.start()
+                        copy.wait()
+            return carry
+        lax.fori_loop(0, pieces, one, 0)
+
+    def spread(j, carry):
+        @pl.when(owner)
+        def _():
+            near_copy(z, j, own_rows(j)).start()
+        return carry
+
+    def spread_u(j, carry):
+        near_copy_u(z, j, own_rows_u(j)).start()
+        return carry
+
+    def step(t, carry):
+        for place in chips:
+            @pl.when(chip == place[0] * 4 + place[1])
+            def _():
+                for hop in incoming[place]:
+                    block, p, q, first, last, t0 = hop
+
+                    @pl.when((t >= t0 + LAG) & (t < t0 + LAG + last - first))
+                    def _():
+                        j = t - (t0 + LAG) + first
+                        each(block, j, lambda columns: hop_copy(hop, 0, j, columns).wait_recv())
+                        if block[0] == "u":
+                            near_copy_u(block[1], j).start()
+                        elif block in needs[place]:
+                            near_copy(slots[place][block], j).start()
+                for hop, number in outgoing[place]:
+                    block, p, q, first, last, t0 = hop
+
+                    @pl.when((t >= t0) & (t < t0 + last - first))
+                    def _():
+                        j = t - t0 + first
+                        each(block, j, lambda columns: hop_copy(hop, number, j, columns).start())
+
+        def consume(m, carry):
+            begin = jnp.int32(-1000)
+            for level in range(4):
+                begin = jnp.where(m == level, begins[level], begin)
+            ago = t - begin
+
+            @pl.when((ago >= 0) & (ago < pieces) & (lax.rem(ago, 2) == 0))
+            def _():
+                slot_b = jnp.where(c == z, m, 4 + m)
+                for i in range(2):
+                    near_arrival(m, ago + i).wait_recv()
+
+                    @pl.when(c != z)
+                    def _():
+                        near_arrival(slot_b, ago + i).wait_recv()
+                loads = []
+                cols = pl.ds(pl.multiple_of(k * tall, tall), tall)
+                for core in range(2):
+                    at_a = pl.ds(pl.multiple_of((m * 2 + core) * rows + ago * h, 2 * h), 2 * h)
+                    at_b = pl.ds(pl.multiple_of((slot_b * 2 + core) * rows + ago * h, 2 * h), 2 * h)
+                    into = pl.ds(core * 2 * h, 2 * h)
+                    loads.append(pltpu.make_async_copy(x_ref.at[at_a, :], a_buf.at[into, :], local.at[2 + core]))
+                    loads.append(pltpu.make_async_copy(x_ref.at[at_b, cols], b_buf.at[into, :], local.at[4 + core]))
+                for copy in loads:
+                    copy.start()
+                for copy in loads:
+                    copy.wait()
+                tile = min(256, tall)
+
+                def rows_of(i, carry):
+                    at = pl.ds(pl.multiple_of(i * tile, tile), tile)
+                    acc[at, :] += lax.dot_general(
+                        b_buf[:, at], a_buf[...], (((0,), (0,)), ((), ())), preferred_element_type=jnp.float32)
+                    return carry
+                lax.fori_loop(0, tall // tile, rows_of, 0)
+            return carry
+        lax.fori_loop(0, 4, consume, 0)
+        return carry
+
+    begins = []
+    for m in range(4):
+        begin = jnp.int32(-1000)
+        for place in chips:
+            if (place, m) in due:
+                begin = jnp.where(chip == place[0] * 4 + place[1], due[place, m], begin)
+        begins.append(begin)
+
+    lax.fori_loop(0, pieces, spread, 0)
+    lax.fori_loop(0, coupling_pieces, spread_u, 0)
+    own = pltpu.make_async_copy(f_ref, stage, local.at[0])
+    keep = pltpu.make_async_copy(stage, x_ref.at[pl.ds(pl.multiple_of((z * 2 + k) * rows, rows), rows), :], local.at[0])
+
+    own_u = pltpu.make_async_copy(u_ref, stage_u, local.at[1])
+    keep_u = pltpu.make_async_copy(stage_u, ub_ref.at[r], local.at[1])
+
+    @pl.when(owner)
+    def _():
+        own.start()
+    acc[...] = jnp.zeros_like(acc)
+    for place in chips:
+        filled = [slots[place][b] for b in needs[place] if b[0] == b[1] and b != place]
+        for slot in filled:
+            @pl.when(chip == place[0] * 4 + place[1])
+            def _():
+                fill(slot, 0)
+
+    @pl.when(owner)
+    def _():
+        own.wait()
+        keep.start()
+        keep.wait()
+    own_u.start()
+    own_u.wait()
+    keep_u.start()
+    keep_u.wait()
+    lax.fori_loop(0, steps, step, 0)
+    out = pltpu.make_async_copy(acc, g_ref, local.at[0])
+    out.start()
+
+    def settle(j, carry):
+        @pl.when(owner)
+        def _():
+            near_copy(z, j, own_rows(j)).wait_send()
+        return carry
+    lax.fori_loop(0, pieces, settle, 0)
+
+    def settle_u(j, carry):
+        for level in range(4):
+            near_copy_u(level, j).wait_send()
+            at = pl.ds(pl.multiple_of(j * hu, hu), hu)
+            ref = ub_ref.at[level * 2 + 1 - k, at, :]
+            remote(ref, ref, near_u.at[level, j], recv_near_u.at[level, j], r, c).wait_recv()
+        return carry
+    lax.fori_loop(0, coupling_pieces, settle_u, 0)
+    for place in chips:
+        @pl.when(chip == place[0] * 4 + place[1])
+        def _():
+            for hop, number in outgoing[place]:
+                def sent(j, carry):
+                    each(hop[0], j, lambda columns: hop_copy(hop, number, j, columns).wait_send())
+                    return carry
+                lax.fori_loop(hop[3], hop[4], sent, 0)
+            for hop in incoming[place]:
+                if hop[0][0] != "u" and hop[0] in needs[place]:
+                    def passed(j, carry):
+                        near_copy(slots[place][hop[0]], j).wait_send()
+                        return carry
+                    lax.fori_loop(hop[3], hop[4], passed, 0)
+    out.wait()
+
+
+def stream(factor, coupling, n_row, n_col):
+    rows, width = factor.shape
+    depth, narrow = coupling.shape
+    pieces, coupling_pieces = 16, 4
+    hops = plan(pieces, coupling_pieces)[0]
+    out_count = max(sum(hop[1] == chip and hop[0][0] != "u" for hop in hops) for chip in {h[1] for h in hops})
+    out_count_u = max(sum(hop[1] == chip and hop[0][0] == "u" for hop in hops) for chip in {h[1] for h in hops})
+    tall = width // 2
+    h = rows // pieces
+    dma = pltpu.SemaphoreType.DMA
+    return pl.pallas_call(
+        functools.partial(stream_kernel, pieces, coupling_pieces),
+        out_shape=(
+            jax.ShapeDtypeStruct((8 * 2 * rows, width), factor.dtype),
+            jax.ShapeDtypeStruct((n_row, depth, narrow), coupling.dtype),
+            jax.ShapeDtypeStruct((tall, width), jnp.float32),
+        ),
+        in_specs=[pl.BlockSpec(memory_space=pl.ANY)] * 2,
+        out_specs=[pl.BlockSpec(memory_space=pl.ANY)] * 3,
+        scratch_shapes=[
+            dma((out_count, pieces)),
+            dma((out_count_u, coupling_pieces)),
+            dma((8, pieces)),
+            dma((4, coupling_pieces)),
+            dma((8, pieces)),
+            dma((4, coupling_pieces)),
+            dma((8, pieces)),
+            dma((4, coupling_pieces)),
+            dma((6,)),
+            pltpu.VMEM((tall, width), jnp.float32),
+            pltpu.VMEM((4 * h, width), factor.dtype),
+            pltpu.VMEM((4 * h, tall), factor.dtype),
+            pltpu.VMEM((rows, width), factor.dtype),
+            pltpu.VMEM((depth, narrow), coupling.dtype),
+            pltpu.VMEM((h, width), factor.dtype),
+        ],
+        compiler_params=pltpu.CompilerParams(has_side_effects=True, vmem_limit_bytes=48 * 1024 * 1024),
+        cost_estimate=pl.CostEstimate(flops=0, bytes_accessed=rows * width * 64, transcendentals=0),
+    )(factor, coupling)
+
+
 def exchange_kernel(n_col, part_ref, out_ref, send, recv):
     r, c = lax.axis_index("row"), lax.axis_index("col")
     depth = out_ref.shape[1]
@@ -251,7 +618,7 @@
     )(part)
 
 
-def body(n_row, n_col, factor, sel_tiles, coupling):
+def general(n_row, n_col, factor, coupling):
     rows_here = factor.shape[0]
     row_index, col_index = lax.axis_index("row"), lax.axis_index("col")
     cores = n_row // n_col
@@ -271,11 +638,27 @@
         partner,
     )
     rounded = gram.astype(jnp.bfloat16)
-    global_rows = row_index * rows_here + jnp.arange(rows_here, dtype=jnp.int32)
-    member = jnp.any((global_rows // TILE)[:, None] == sel_tiles[None, :], axis=1)
     part = lax.dot_general(
         coupling_full, rounded, (((0,), (1,)), ((), ())), preferred_element_type=jnp.float32
     ).astype(jnp.bfloat16)
+    return gram, part
+
+
+def body(n_row, n_col, factor, sel_tiles, coupling):
+    rows_here = factor.shape[0]
+    row_index, col_index = lax.axis_index("row"), lax.axis_index("col")
+    cores = n_row // n_col
+    if (n_row, n_col) == (8, 4):
+        _, pieces, gram = stream(factor, coupling, n_row, n_col)
+        rounded = gram.astype(jnp.bfloat16)
+        part = lax.dot_general(
+            pieces, rounded, (((1,), (1,)), ((), ())), preferred_element_type=jnp.float32
+        ).astype(jnp.bfloat16)
+        part = part.reshape(-1, part.shape[-1])
+    else:
+        gram, part = general(n_row, n_col, factor, coupling)
+    global_rows = row_index * rows_here + jnp.arange(rows_here, dtype=jnp.int32)
+    member = jnp.any((global_rows // TILE)[:, None] == sel_tiles[None, :], axis=1)
     depth = part.shape[0] // n_col
     arrived = exchange(part, n_col)
     summed = lax.dynamic_slice_in_dim(part, col_index * depth, depth, 0).astype(jnp.float32)

time: 500 us -> 401 us (0.80)
  Pallas kernels: 421 us -> 368 us
  matrix products: 59.1 us -> 15.2 us
  between operations: 14.1 us -> 0.68 us
  local copies, waits for them, and re-layouts: 0.01 us -> 11.3 us
    pallas_call x1, Pallas kernels: 373 us -> 276 us  [stream(): pl.pallas_call(functools.partial(stream_kernel, pieces, coupling_pieces),...]
    pallas_call x1, Pallas kernels: 48.3 us -> 92.5 us  [exchange(): pl.pallas_call(functools.partial(exchange_kernel, n_col), out_shape=jax.S...]
    dot_general x2 -> x1, matrix products: 59.1 us -> 15.2 us  [body(): lax.dot_general(pieces, rounded, (((1,), (1,)), ((), ())), preferred_elem...]
    unnamed x2 -> x7, local copies, waits for them, and re-layouts: 0.01 us -> 11.3 us
  transfers between devices with their start and end apart: 1 -> 0, of which waited for: 0 -> 0; matrix products, arithmetic and copies ran while one was open for 9% -> 0% of each run, Pallas kernels for 75% -> 0%
where the time goes in v1:
time: 401 us; the launch traced here: 400 us
  Pallas kernels  368 us (92%)
  matrix products  15.2 us (4%)
  local copies, waits for them, and re-layouts  11.3 us (3%)
  other arithmetic  4.49 us (1%)
    pallas_call x1, Pallas kernels, stream(): pl.pallas_call(functools.partial(stream_kernel, pieces, coupling_pieces),...  276 us
    pallas_call x1, Pallas kernels, exchange(): pl.pallas_call(functools.partial(exchange_kernel, n_col), out_shape=jax.S...  92.5 us
    dot_general x1, matrix products, body(): lax.dot_general(pieces, rounded, (((1,), (1,)), ((), ())), preferred_elem...  15.2 us
    unnamed x7, local copies, waits for them, and re-layouts  11.3 us

profile of v1, /device:TPU:0, one launch (start us, length us, event | category | flops | bytes accessed | tf_op | source)
XLA Modules:
  0.0 400.1 jit_solution(4116098472470296118)
XLA Ops:
  0.6 0.0 copy-start
  0.6 2.2 copy-done
  2.8 0.0 copy-start.1
  2.8 1.2 copy-done.1
  4.0 276.0 %shard_map.50 = (bf16[16384,2048]{1,0:T(8,128)(2,1)}, bf16[8,2048,256]{2,1,0:T(8,128)(2,1)}, f32[1024,2048]{1,0:T(8,128)}) custom-call(bf16[1024,2048]{1,0:T(8,128)(2,1)S(1)} %copy-done, bf16[2048,256]{1,0:T(8,128)(2,1)S(1)} %copy-done.1), custom_call_target="tpu_custom_call" | custom-call | bytes 134217728 | tf_op jit(solution)/shard_map/pallas_call | solution.py:557
  280.0 15.2 %fusion.3 = bf16[8,256,1024]{2,1,0:T(8,128)(2,1)} fusion(bf16[8,2048,256]{2,1,0:T(8,128)(2,1)} %get-tuple-element.5, f32[1024,2048]{1,0:T(8,128)} %get-tuple-element.8), kind=kOutput, calls=%fused_computation.3 | convolution fusion | flops 8594128896 | bytes 20971520 | tf_op jit(solution)/shard_map/dot_general | solution.py:654
  295.2 0.0 copy-start.2
  295.2 92.5 %shard_map.51 = bf16[3,512,1024]{2,1,0:T(8,128)(2,1)} custom-call(bf16[2048,1024]{1,0:T(8,128)(2,1)} %bitcast.16), custom_call_target="tpu_custom_call" | custom-call | tf_op jit(solution)/shard_map/pallas_call | solution.py:611
  387.8 0.0 copy-done.2
  387.8 0.1 compare_reduce_fusion
  387.9 4.4 %fusion.7 = f32[512,1024]{1,0:T(8,128)} fusion(bf16[3,512,1024]{2,1,0:T(8,128)(2,1)} %shard_map.51, bf16[2048,1024]{1,0:T(8,128)(2,1)} %bitcast.17, s32[]{:T(128)S(6)} %select_n.17, pred[1024]{0:T(1024)(128)(4,1)S(1)} %compare_reduce_fusion), kind=kLoop, calls=%fused_computation.6 | loop fusion | flops 4718592 | bytes 6292484 | tf_op jit(solution)/shard_map/jit(_where)/select_n | solution.py:667
  392.3 7.9 %copy.9 = f32[1024,2048]{1,0:T(8,128)} copy(f32[1024,2048]{1,0:T(8,128)} %get-tuple-element.8) | data formatting | bytes 16777216
  (1 shorter events, 0.0 us)
Async XLA Ops:
  0.6 2.2 copy-start
  2.8 1.2 copy-start.1
  295.2 92.5 %copy-start.2 = (s32[32]{0:T(128)S(1)}, s32[32]{0:T(128)}, u32[]{:S(2)}) copy-start(s32[32]{0:T(128)} %param.4) | copy-start | bytes 388

commit v2 on v1

--- a/solution.py
+++ b/solution.py
@@ -219,29 +219,33 @@
 
 
 LAG = 2
+G = ("g", 1, 0)
 
 
 def block_flows(pieces):
     half = pieces // 2
     found = []
 
-    def add(block, hops, first=0, last=pieces):
-        found.append((block, block, hops, first, last))
-
-    side = [((3, 1), (2, 1)), ((2, 1), (1, 1)), ((1, 1), (1, 3)), ((1, 3), (1, 2)), ((1, 2), (1, 0))]
-    add((3, 3), [((3, 3), (2, 3)), ((2, 3), (1, 3)), ((1, 3), (0, 3)), ((3, 3), (3, 1)), ((3, 3), (3, 2)),
-                 ((3, 2), (3, 0))])
-    add((3, 2), [((3, 2), (2, 2)), ((2, 2), (2, 3)), ((2, 3), (2, 1)), ((2, 2), (2, 0)), ((2, 2), (1, 2)),
-                 ((1, 2), (0, 2))])
-    add((3, 1), side + [((1, 1), (0, 1))], 0, half)
-    add((3, 1), side + [((1, 3), (0, 3)), ((0, 3), (0, 1))], half, pieces)
-    add((3, 0), [((3, 0), (2, 0)), ((2, 0), (2, 1)), ((2, 1), (2, 3)), ((2, 3), (1, 3)), ((1, 3), (0, 3)),
-                 ((0, 3), (0, 1)), ((0, 1), (0, 0)), ((0, 3), (0, 2)), ((2, 0), (1, 0))])
-    add((2, 0), [((2, 0), (1, 0)), ((1, 0), (0, 0)), ((0, 0), (0, 1)), ((0, 0), (0, 2))])
-    add((1, 0), [((1, 0), (0, 0)), ((0, 0), (0, 1))])
-    add((2, 1), [((2, 1), (1, 1)), ((1, 1), (0, 1)), ((1, 1), (1, 0)), ((1, 0), (1, 2))])
-    add((1, 1), [((1, 1), (0, 1)), ((1, 1), (1, 0))])
-    add((2, 2), [((2, 2), (2, 3)), ((2, 3), (2, 1)), ((2, 2), (2, 0)), ((2, 2), (1, 2)), ((1, 2), (0, 2))])
+    def add(block, source, hops, first=0, last=pieces):
+        found.append((block, source, hops, first, last))
+
+    add((3, 3), (3, 3), [((3, 3), (2, 3)), ((2, 3), (1, 3)), ((1, 3), (0, 3)), ((3, 3), (3, 1)), ((3, 3), (3, 2)),
+                         ((3, 2), (3, 0))])
+    add((3, 2), (3, 2), [((3, 2), (2, 2)), ((2, 2), (2, 3)), ((2, 3), (2, 1)), ((2, 2), (2, 0)), ((2, 2), (1, 2)),
+                         ((1, 2), (0, 2))])
+    add((3, 1), (3, 1), [((3, 1), (2, 1)), ((2, 1), (2, 0)), ((2, 0), (1, 0)), ((1, 0), (1, 1)), ((1, 1), (1, 3)),
+                         ((1, 3), (1, 2))], 0, half)
+    add((3, 1), (3, 1), [((3, 1), (2, 1)), ((2, 1), (1, 1)), ((1, 1), (1, 3)), ((1, 3), (1, 2)), ((1, 2), (1, 0))],
+        half, pieces)
+    add((3, 0), (3, 0), [((3, 0), (2, 0)), ((2, 0), (2, 1)), ((2, 1), (2, 3)), ((2, 3), (1, 3)), ((1, 3), (1, 2)),
+                         ((1, 2), (1, 0)), ((1, 3), (0, 3)), ((0, 3), (0, 2)), ((0, 2), (0, 0))])
+    add((2, 0), (2, 0), [((2, 0), (1, 0)), ((1, 0), (1, 1)), ((1, 1), (0, 1)), ((0, 1), (0, 0)), ((0, 0), (0, 2))])
+    add((1, 0), (1, 0), [((1, 0), (0, 0))])
+    add((2, 1), (2, 1), [((2, 1), (1, 1)), ((1, 1), (1, 0)), ((1, 0), (1, 2))])
+    add((1, 1), (1, 1), [((1, 1), (1, 0))])
+    add((2, 2), (2, 2), [((2, 2), (2, 3)), ((2, 3), (2, 1)), ((2, 2), (2, 0)), ((2, 2), (1, 2)), ((1, 2), (0, 2))])
+    add(G, (1, 0), [((1, 0), (0, 0)), ((0, 0), (0, 1))], 0, half)
+    add(G, (1, 0), [((1, 0), (1, 1)), ((1, 1), (0, 1))], half, pieces)
     return found
 
 
@@ -254,16 +258,22 @@
     return found
 
 
-ORDER = [6, 8, 5, 2, 23, 9, 4, 11, 25, 18, 1, 3, 10, 20, 12, 13, 19, 0, 7, 17, 15, 16, 14, 22, 24, 21]
+ORDER = [3, 4, 19, 12, 0, 20, 23, 22, 21, 5, 25, 2, 13, 6, 16, 26, 27, 24, 1, 7, 18, 15, 17, 8, 9, 14, 10, 11]
 
 
 @functools.cache
 def plan(pieces, coupling_pieces):
     flows = block_flows(pieces) + coupling_flows(coupling_pieces)
-    busy, hops = {}, []
+    chips = [(z, c) for z in range(4) for c in range(4)]
+    pairs = [(chip, m) for chip in chips if chip != (0, 1) for m in range(max(chip), 4)]
+    busy, hops, due = {}, [], {}
+    final = None
     for index in ORDER:
         block, source, route, first, last = flows[index]
-        n, at = last - first, {source: 0}
+        if block == G and final is None:
+            due = ready_steps(pieces, hops, pairs)
+            final = max(d for key, d in due.items() if key[0] == (1, 0)) + pieces // 4
+        n, at = last - first, {source: final + 1 if block == G else 0}
         for p, q in route:
             t, used = at[p], busy.setdefault((p, q), [])
             while any(t < e and s < t + n for s, e in used):
@@ -271,37 +281,42 @@
             used.append((t, t + n))
             at[q] = t + LAG
             hops.append((block, p, q, first, last, t))
-    chips = [(z, c) for z in range(4) for c in range(4)]
     slots = {chip: {} for chip in chips}
     needs = {chip: set() for chip in chips}
-    for z, c in chips:
-        for m in range(max(z, c), 4):
-            slots[z, c][m, c] = m
-            needs[z, c].add((m, c))
-            if c != z:
-                slots[z, c][m, z] = 4 + m
-                needs[z, c].add((m, z))
+    for chip, m in pairs:
+        z, c = chip
+        slots[chip][m, c] = m
+        needs[chip].add((m, c))
+        if c != z:
+            slots[chip][m, z] = 4 + m
+            needs[chip].add((m, z))
     for block, p, q, first, last, t in hops:
-        if block[0] != "u" and block not in slots[q]:
-            slots[q][block] = min(set(range(8)) - set(slots[q].values()))
-    due = {}
-    for chip in chips:
+        for chip in (p, q):
+            if block[0] != "u" and block not in slots[chip] and block != chip:
+                slots[chip][block] = min(set(range(8)) - set(slots[chip].values()))
+    steps = max([t + last - first + LAG for block, p, q, first, last, t in hops] + [d + pieces // 4 for d in due.values()] + [final + 1])
+    return hops, slots, needs, due, steps, final
+
+
+def ready_steps(pieces, hops, pairs):
+    due, group = {}, pieces // 8
+    for chip, m in pairs:
         z, c = chip
         ready = {(z, c): [1] * pieces}
         for block, p, q, first, last, t in hops:
             if q == chip:
                 for j in range(first, last):
                     ready.setdefault(block, [None] * pieces)[j] = t + LAG + j - first
-        for m in range(max(z, c), 4):
-            both = [ready[m, c], ready[m, z]]
-            due[chip, m] = 1 + max(max(b[2 * j], b[2 * j + 1]) - 2 * j for b in both for j in range(pieces // 2))
-    steps = max([t + last - first + LAG for block, p, q, first, last, t in hops] + [d + pieces for d in due.values()])
-    return hops, slots, needs, due, steps
+        both = [ready[m, c], ready[m, z]]
+        for part in range(4):
+            begin = part * (pieces // 4)
+            due[chip, m, part] = 1 + max(b[begin + j] - j // group * group for b in both for j in range(pieces // 4))
+    return due
 
 
 def stream_kernel(pieces, coupling_pieces, f_ref, u_ref, x_ref, ub_ref, g_ref, send, send_u, near, near_u, recv,
-                  recv_u, recv_near, recv_near_u, local, acc, a_buf, b_buf, stage, stage_u, zeros):
-    hops, slots, needs, due, steps = plan(pieces, coupling_pieces)
+                  recv_u, recv_near, recv_near_u, turn, local, acc, a_buf, b_buf, stage, stage_u, zeros, flipped):
+    hops, slots, needs, due, steps, final = plan(pieces, coupling_pieces)
     rows, width = f_ref.shape
     depth, narrow = u_ref.shape
     h, hu, quarter = rows // pieces, depth // coupling_pieces, width // 4
@@ -410,6 +425,33 @@
         near_copy_u(z, j, own_rows_u(j)).start()
         return carry
 
+    def flip():
+        slot = slots[1, 0][G]
+        tile = min(256, width)
+
+        def turned(i, carry):
+            at = pl.ds(pl.multiple_of(i * tile, tile), tile)
+            flipped[at, :] = acc[:, at].T.astype(flipped.dtype)
+            return carry
+        lax.fori_loop(0, width // tile, turned, 0)
+        cols = pl.ds(pl.multiple_of(k * tall, tall), tall)
+        kept = []
+        for half in range(2):
+            at = pl.ds((slot * 2 + half) * rows, rows)
+            kept.append(pltpu.make_async_copy(flipped.at[pl.ds(half * rows, rows), :], x_ref.at[at, cols],
+                                              local.at[half]))
+        for copy in kept:
+            copy.start()
+        for copy in kept:
+            copy.wait()
+        at = pl.ds(pl.multiple_of((slot * 2 + 1 - k) * rows, rows), rows)
+        pass_on = remote(x_ref.at[at, cols], x_ref.at[at, cols], turn.at[0], turn.at[1], z * 2 + 1 - k, c)
+        pass_on.start()
+        pass_on.wait_send()
+        at = pl.ds(pl.multiple_of((slot * 2 + k) * rows, rows), rows)
+        cols = pl.ds(pl.multiple_of((1 - k) * tall, tall), tall)
+        remote(x_ref.at[at, cols], x_ref.at[at, cols], turn.at[0], turn.at[1], r, c).wait_recv()
+
     def step(t, carry):
         for place in chips:
             @pl.when(chip == place[0] * 4 + place[1])
@@ -433,14 +475,16 @@
                         j = t - t0 + first
                         each(block, j, lambda columns: hop_copy(hop, number, j, columns).start())
 
-        def consume(m, carry):
+        def consume(entry, carry):
             begin = jnp.int32(-1000)
-            for level in range(4):
-                begin = jnp.where(m == level, begins[level], begin)
-            ago = t - begin
-
-            @pl.when((ago >= 0) & (ago < pieces) & (lax.rem(ago, 2) == 0))
+            for index in range(16):
+                begin = jnp.where(entry == index, begins[index], begin)
+            m, part = entry // 4, lax.rem(entry, 4)
+            past = t - begin
+
+            @pl.when((past >= 0) & (past < pieces // 4) & (lax.rem(past, 2) == 0))
             def _():
+                ago = past + part * (pieces // 4)
                 slot_b = jnp.where(c == z, m, 4 + m)
                 for i in range(2):
                     near_arrival(m, ago + i).wait_recv()
@@ -469,15 +513,19 @@
                     return carry
                 lax.fori_loop(0, tall // tile, rows_of, 0)
             return carry
-        lax.fori_loop(0, 4, consume, 0)
+        lax.fori_loop(0, 16, consume, 0)
+
+        @pl.when((chip == 4) & (t == final))
+        def _():
+            flip()
         return carry
 
     begins = []
-    for m in range(4):
+    for index in range(16):
         begin = jnp.int32(-1000)
         for place in chips:
-            if (place, m) in due:
-                begin = jnp.where(chip == place[0] * 4 + place[1], due[place, m], begin)
+            if (place, index // 4, index % 4) in due:
+                begin = jnp.where(chip == place[0] * 4 + place[1], due[place, index // 4, index % 4], begin)
         begins.append(begin)
 
     lax.fori_loop(0, pieces, spread, 0)
@@ -509,6 +557,20 @@
     keep_u.start()
     keep_u.wait()
     lax.fori_loop(0, steps, step, 0)
+
+    @pl.when(chip == 1)
+    def _():
+        at = pl.ds(pl.multiple_of((slots[0, 1][G] * 2 + k) * rows, rows), rows)
+        load = pltpu.make_async_copy(x_ref.at[at, :], stage, local.at[0])
+        load.start()
+        load.wait()
+        tile = min(128, tall)
+
+        def widen(i, carry):
+            at = pl.ds(pl.multiple_of(i * tile, tile), tile)
+            acc[at, :] = stage[at, :].astype(jnp.float32)
+            return carry
+        lax.fori_loop(0, tall // tile, widen, 0)
     out = pltpu.make_async_copy(acc, g_ref, local.at[0])
     out.start()
 
@@ -572,6 +634,7 @@
             dma((4, coupling_pieces)),
             dma((8, pieces)),
             dma((4, coupling_pieces)),
+            dma((2,)),
             dma((6,)),
             pltpu.VMEM((tall, width), jnp.float32),
             pltpu.VMEM((4 * h, width), factor.dtype),
@@ -579,10 +642,48 @@
             pltpu.VMEM((rows, width), factor.dtype),
             pltpu.VMEM((depth, narrow), coupling.dtype),
             pltpu.VMEM((h, width), factor.dtype),
+            pltpu.VMEM((width, tall), factor.dtype),
         ],
-        compiler_params=pltpu.CompilerParams(has_side_effects=True, vmem_limit_bytes=48 * 1024 * 1024),
+        compiler_params=pltpu.CompilerParams(has_side_effects=True, vmem_limit_bytes=63 * 1024 * 1024),
         cost_estimate=pl.CostEstimate(flops=0, bytes_accessed=rows * width * 64, transcendentals=0),
     )(factor, coupling)
+
+
+def finish_kernel(g_ref, u_ref, gram_ref, part_ref):
+    gram_ref[...] = g_ref[...]
+    rounded = g_ref[...].astype(u_ref.dtype)
+    narrow = u_ref.shape[2]
+
+    def one(i, carry):
+        product = jnp.dot(rounded, u_ref[i], preferred_element_type=jnp.float32)
+        part_ref[pl.ds(pl.multiple_of(i * narrow, narrow), narrow), :] = product.T.astype(part_ref.dtype)
+        return carry
+    lax.fori_loop(0, u_ref.shape[0], one, 0)
+
+
+def finish(gram, coupling):
+    tall, width = gram.shape
+    count, depth, narrow = coupling.shape
+    tile = min(256, tall)
+    return pl.pallas_call(
+        finish_kernel,
+        grid=(tall // tile,),
+        out_shape=(
+            jax.ShapeDtypeStruct((tall, width), jnp.float32),
+            jax.ShapeDtypeStruct((count * narrow, tall), coupling.dtype),
+        ),
+        in_specs=[
+            pl.BlockSpec((tile, width), lambda i: (i, 0)),
+            pl.BlockSpec((count, depth, narrow), lambda i: (0, 0, 0)),
+        ],
+        out_specs=(
+            pl.BlockSpec((tile, width), lambda i: (i, 0)),
+            pl.BlockSpec((count * narrow, tile), lambda i: (0, i)),
+        ),
+        compiler_params=pltpu.CompilerParams(vmem_limit_bytes=63 * 1024 * 1024),
+        cost_estimate=pl.CostEstimate(
+            flops=2 * tall * width * count * narrow, bytes_accessed=tall * width * 16, transcendentals=0),
+    )(gram, coupling)
 
 
 def exchange_kernel(n_col, part_ref, out_ref, send, recv):
@@ -650,11 +751,7 @@
     cores = n_row // n_col
     if (n_row, n_col) == (8, 4):
         _, pieces, gram = stream(factor, coupling, n_row, n_col)
-        rounded = gram.astype(jnp.bfloat16)
-        part = lax.dot_general(
-            pieces, rounded, (((1,), (1,)), ((), ())), preferred_element_type=jnp.float32
-        ).astype(jnp.bfloat16)
-        part = part.reshape(-1, part.shape[-1])
+        gram, part = finish(gram, pieces)
     else:
         gram, part = general(n_row, n_col, factor, coupling)
     global_rows = row_index * rows_here + jnp.arange(rows_here, dtype=jnp.int32)

time: 401 us -> 372 us (0.928)
  matrix products: 15.2 us -> 0 us
  local copies, waits for them, and re-layouts: 11.3 us -> 0.01 us
    pallas_call x1, Pallas kernels: 92.5 us -> 56.5 us  [exchange(): pl.pallas_call(functools.partial(exchange_kernel, n_col), out_shape=jax.S...]
    pallas_call x0 -> x1, Pallas kernels: none -> 23.3 us  [finish(): pl.pallas_call(finish_kernel, grid=(tall // tile,), out_shape=(jax.ShapeD...]
    dot_general x1 -> x0, matrix products: 15.2 us -> none  [body(): lax.dot_general(pieces, rounded, (((1,), (1,)), ((), ())), preferred_elem...]
    unnamed x7 -> x2, local copies, waits for them, and re-layouts: 11.3 us -> 0.01 us
    pallas_call x1, Pallas kernels: 276 us -> 286 us  [stream(): pl.pallas_call(functools.partial(stream_kernel, pieces, coupling_pieces),...]
where the time goes in v2:
time: 372 us; the launch traced here: 371 us
  Pallas kernels  366 us (98%)
  other arithmetic  4.49 us (1%)
    pallas_call x1, Pallas kernels, stream(): pl.pallas_call(functools.partial(stream_kernel, pieces, coupling_pieces),...  286 us
    pallas_call x1, Pallas kernels, exchange(): pl.pallas_call(functools.partial(exchange_kernel, n_col), out_shape=jax.S...  56.5 us
    pallas_call x1, Pallas kernels, finish(): pl.pallas_call(finish_kernel, grid=(tall // tile,), out_shape=(jax.ShapeD...  23.3 us

profile of v2, /device:TPU:0, one launch (start us, length us, event | category | flops | bytes accessed | tf_op | source)
XLA Modules:
  0.0 371.2 jit_solution(1495501523632737865)
XLA Ops:
  0.6 286.3 %shard_map.50 = (bf16[16384,2048]{1,0:T(8,128)(2,1)}, bf16[8,2048,256]{2,1,0:T(8,128)(2,1)}, f32[1024,2048]{1,0:T(8,128)}) custom-call(bf16[1024,2048]{1,0:T(8,128)(2,1)} %f_ref.1, bf16[2048,256]{1,0:T(8,128)(2,1)} %u_ref.1), custom_call_target="tpu_custom_call" | custom-call | bytes 134217728 | tf_op jit(solution)/shard_map/pallas_call | solution.py:619
  286.9 23.3 %shard_map.51 = (f32[1024,2048]{1,0:T(8,128)}, bf16[2048,1024]{1,0:T(8,128)(2,1)}) custom-call(f32[1024,2048]{1,0:T(8,128)} %get-tuple-element.6.g_ref, bf16[8,2048,256]{2,1,0:T(8,128)(2,1)} %get-tuple-element.7.u_ref), custom_call_target="tpu_custom_call" | custom-call | flops 8589934592 | bytes 33554432 | tf_op jit(solution)/shard_map/pallas_call | solution.py:668
  310.2 0.0 copy-start
  310.2 56.5 %shard_map.52 = bf16[3,512,1024]{2,1,0:T(8,128)(2,1)} custom-call(bf16[2048,1024]{1,0:T(8,128)(2,1)} %get-tuple-element.9.part_ref), custom_call_target="tpu_custom_call" | custom-call | tf_op jit(solution)/shard_map/pallas_call | solution.py:712
  366.7 0.0 copy-done
  366.7 0.1 compare_reduce_fusion
  366.8 4.4 %fusion.1 = f32[512,1024]{1,0:T(8,128)} fusion(bf16[3,512,1024]{2,1,0:T(8,128)(2,1)} %shard_map.52, bf16[2048,1024]{1,0:T(8,128)(2,1)} %get-tuple-element.9.part_ref, s32[]{:T(128)S(6)} %select_n.17, pred[1024]{0:T(1024)(128)(4,1)S(1)} %compare_reduce_fusion), kind=kLoop, calls=%fused_computation.2 | loop fusion | flops 4718592 | bytes 6292484 | tf_op jit(solution)/shard_map/jit(_where)/select_n | solution.py:764
  (1 shorter events, 0.0 us)
Async XLA Ops:
  310.2 56.5 %copy-start = (s32[32]{0:T(128)S(1)}, s32[32]{0:T(128)}, u32[]{:S(2)}) copy-start(s32[32]{0:T(128)} %param.4) | copy-start | bytes 388

commit v3 on v2

--- a/solution.py
+++ b/solution.py
@@ -315,7 +315,7 @@
 
 
 def stream_kernel(pieces, coupling_pieces, f_ref, u_ref, x_ref, ub_ref, g_ref, send, send_u, near, near_u, recv,
-                  recv_u, recv_near, recv_near_u, turn, local, acc, a_buf, b_buf, stage, stage_u, zeros, flipped):
+                  recv_u, recv_near, recv_near_u, turn, blank, local, acc, a_buf, b_buf, stage, stage_u, zeros, flipped):
     hops, slots, needs, due, steps, final = plan(pieces, coupling_pieces)
     rows, width = f_ref.shape
     depth, narrow = u_ref.shape
@@ -400,20 +400,23 @@
 
     zeros[...] = jnp.zeros_like(zeros)
 
-    def fill(slot, begin):
+    def fill(slot, act):
         def one(j, carry):
             for condition, columns in shapes((0, 0), j):
                 if columns < width:
-                    copy = pltpu.make_async_copy(
-                        zeros.at[:, pl.ds(0, width - columns)],
-                        x_ref.at[at_rows(slot, k, j), pl.ds(columns, width - columns)], local.at[1])
-
                     @pl.when(condition)
                     def _():
-                        copy.start()
-                        copy.wait()
+                        act(pltpu.make_async_copy(
+                            zeros.at[:, pl.ds(0, width - columns)],
+                            x_ref.at[at_rows(slot, k, j), pl.ds(columns, width - columns)], blank.at[j]))
             return carry
         lax.fori_loop(0, pieces, one, 0)
+
+    def fill_all(act):
+        for place in chips:
+            for block in needs[place]:
+                if block[0] == block[1] and block != place:
+                    pl.when(chip == place[0] * 4 + place[1])(functools.partial(fill, slots[place][block], act))
 
     def spread(j, carry):
         @pl.when(owner)
@@ -424,6 +427,29 @@
     def spread_u(j, carry):
         near_copy_u(z, j, own_rows_u(j)).start()
         return carry
+
+    def loads(m, slot_b, ago, into):
+        cols = pl.ds(pl.multiple_of(k * tall, tall), tall)
+        found = []
+        for core in range(2):
+            at_a = pl.ds(pl.multiple_of((m * 2 + core) * rows + ago * h, 2 * h), 2 * h)
+            at_b = pl.ds(pl.multiple_of((slot_b * 2 + core) * rows + ago * h, 2 * h), 2 * h)
+            half = pl.ds(core * 2 * h, 2 * h)
+            found.append(pltpu.make_async_copy(x_ref.at[at_a, :], a_buf.at[into, half, :], local.at[2 + into * 4 + core]))
+            found.append(pltpu.make_async_copy(x_ref.at[at_b, cols], b_buf.at[into, half, :], local.at[4 + into * 4 + core]))
+        return found
+
+    def multiply(into):
+        for copy in loads(0, 0, 0, into):
+            copy.wait()
+        tile = min(256, tall)
+
+        def rows_of(i, carry):
+            at = pl.ds(pl.multiple_of(i * tile, tile), tile)
+            acc[at, :] += lax.dot_general(
+                b_buf[into, :, at], a_buf[into], (((0,), (0,)), ((), ())), preferred_element_type=jnp.float32)
+            return carry
+        lax.fori_loop(0, tall // tile, rows_of, 0)
 
     def flip():
         slot = slots[1, 0][G]
@@ -476,13 +502,15 @@
                         each(block, j, lambda columns: hop_copy(hop, number, j, columns).start())
 
         def consume(entry, carry):
+            pending, into = carry
             begin = jnp.int32(-1000)
             for index in range(16):
                 begin = jnp.where(entry == index, begins[index], begin)
             m, part = entry // 4, lax.rem(entry, 4)
             past = t - begin
-
-            @pl.when((past >= 0) & (past < pieces // 4) & (lax.rem(past, 2) == 0))
+            ready = (past >= 0) & (past < pieces // 4) & (lax.rem(past, 2) == 0)
+
+            @pl.when(ready)
             def _():
                 ago = past + part * (pieces // 4)
                 slot_b = jnp.where(c == z, m, 4 + m)
@@ -492,33 +520,18 @@
                     @pl.when(c != z)
                     def _():
                         near_arrival(slot_b, ago + i).wait_recv()
-                loads = []
-                cols = pl.ds(pl.multiple_of(k * tall, tall), tall)
-                for core in range(2):
-                    at_a = pl.ds(pl.multiple_of((m * 2 + core) * rows + ago * h, 2 * h), 2 * h)
-                    at_b = pl.ds(pl.multiple_of((slot_b * 2 + core) * rows + ago * h, 2 * h), 2 * h)
-                    into = pl.ds(core * 2 * h, 2 * h)
-                    loads.append(pltpu.make_async_copy(x_ref.at[at_a, :], a_buf.at[into, :], local.at[2 + core]))
-                    loads.append(pltpu.make_async_copy(x_ref.at[at_b, cols], b_buf.at[into, :], local.at[4 + core]))
-                for copy in loads:
+                for copy in loads(m, slot_b, ago, 1 - into):
                     copy.start()
-                for copy in loads:
-                    copy.wait()
-                tile = min(256, tall)
-
-                def rows_of(i, carry):
-                    at = pl.ds(pl.multiple_of(i * tile, tile), tile)
-                    acc[at, :] += lax.dot_general(
-                        b_buf[:, at], a_buf[...], (((0,), (0,)), ((), ())), preferred_element_type=jnp.float32)
-                    return carry
-                lax.fori_loop(0, tall // tile, rows_of, 0)
-            return carry
-        lax.fori_loop(0, 16, consume, 0)
-
-        @pl.when((chip == 4) & (t == final))
+                pl.when(pending == 1)(functools.partial(multiply, into))
+            return jnp.where(ready, 1, pending), jnp.where(ready, 1 - into, into)
+        pending, into = lax.fori_loop(0, 16, consume, carry)
+        last = (chip == 4) & (t == final)
+
+        @pl.when(last)
         def _():
+            pl.when(pending == 1)(functools.partial(multiply, into))
             flip()
-        return carry
+        return jnp.where(last, 0, pending), into
 
     begins = []
     for index in range(16):
@@ -528,35 +541,28 @@
                 begin = jnp.where(chip == place[0] * 4 + place[1], due[place, index // 4, index % 4], begin)
         begins.append(begin)
 
+    own = pltpu.make_async_copy(f_ref, stage, local.at[0])
+    keep = pltpu.make_async_copy(stage, x_ref.at[pl.ds(pl.multiple_of((z * 2 + k) * rows, rows), rows), :], local.at[0])
+    own_u = pltpu.make_async_copy(u_ref, stage_u, local.at[1])
+    keep_u = pltpu.make_async_copy(stage_u, ub_ref.at[r], local.at[1])
+    pl.when(owner)(own.start)
+    own_u.start()
     lax.fori_loop(0, pieces, spread, 0)
     lax.fori_loop(0, coupling_pieces, spread_u, 0)
-    own = pltpu.make_async_copy(f_ref, stage, local.at[0])
-    keep = pltpu.make_async_copy(stage, x_ref.at[pl.ds(pl.multiple_of((z * 2 + k) * rows, rows), rows), :], local.at[0])
-
-    own_u = pltpu.make_async_copy(u_ref, stage_u, local.at[1])
-    keep_u = pltpu.make_async_copy(stage_u, ub_ref.at[r], local.at[1])
-
-    @pl.when(owner)
-    def _():
-        own.start()
+    fill_all(lambda copy: copy.start())
     acc[...] = jnp.zeros_like(acc)
-    for place in chips:
-        filled = [slots[place][b] for b in needs[place] if b[0] == b[1] and b != place]
-        for slot in filled:
-            @pl.when(chip == place[0] * 4 + place[1])
-            def _():
-                fill(slot, 0)
 
     @pl.when(owner)
     def _():
         own.wait()
         keep.start()
-        keep.wait()
-    own_u.start()
     own_u.wait()
     keep_u.start()
+    fill_all(lambda copy: copy.wait())
+    pl.when(owner)(keep.wait)
     keep_u.wait()
-    lax.fori_loop(0, steps, step, 0)
+    pending, turned_to = lax.fori_loop(0, steps, step, (jnp.int32(0), jnp.int32(0)))
+    pl.when(pending == 1)(functools.partial(multiply, turned_to))
 
     @pl.when(chip == 1)
     def _():
@@ -635,10 +641,11 @@
             dma((8, pieces)),
             dma((4, coupling_pieces)),
             dma((2,)),
-            dma((6,)),
+            dma((pieces,)),
+            dma((12,)),
             pltpu.VMEM((tall, width), jnp.float32),
-            pltpu.VMEM((4 * h, width), factor.dtype),
-            pltpu.VMEM((4 * h, tall), factor.dtype),
+            pltpu.VMEM((2, 4 * h, width), factor.dtype),
+            pltpu.VMEM((2, 4 * h, tall), factor.dtype),
             pltpu.VMEM((rows, width), factor.dtype),
             pltpu.VMEM((depth, narrow), coupling.dtype),
             pltpu.VMEM((h, width), factor.dtype),

time: 372 us -> 356 us (0.957)
  Pallas kernels: 366 us -> 351 us
    pallas_call x1, Pallas kernels: 286 us -> 271 us  [stream(): pl.pallas_call(functools.partial(stream_kernel, pieces, coupling_pieces),...]
where the time goes in v3:
time: 356 us
  Pallas kernels  351 us (99%)
  other arithmetic  4.49 us (1%)
    pallas_call x1, Pallas kernels, stream(): pl.pallas_call(functools.partial(stream_kernel, pieces, coupling_pieces),...  271 us
    pallas_call x1, Pallas kernels, exchange(): pl.pallas_call(functools.partial(exchange_kernel, n_col), out_shape=jax.S...  56.5 us
    pallas_call x1, Pallas kernels, finish(): pl.pallas_call(finish_kernel, grid=(tall // tile,), out_shape=(jax.ShapeD...  23.3 us

profile of v3, /device:TPU:0, one launch (start us, length us, event | category | flops | bytes accessed | tf_op | source)
XLA Modules:
  0.0 356.2 jit_solution(8067125696244780816)
XLA Ops:
  0.6 271.3 %shard_map.50 = (bf16[16384,2048]{1,0:T(8,128)(2,1)}, bf16[8,2048,256]{2,1,0:T(8,128)(2,1)}, f32[1024,2048]{1,0:T(8,128)}) custom-call(bf16[1024,2048]{1,0:T(8,128)(2,1)} %f_ref.1, bf16[2048,256]{1,0:T(8,128)(2,1)} %u_ref.1), custom_call_target="tpu_custom_call" | custom-call | bytes 134217728 | tf_op jit(solution)/shard_map/pallas_call | solution.py:625
  271.9 23.3 %shard_map.51 = (f32[1024,2048]{1,0:T(8,128)}, bf16[2048,1024]{1,0:T(8,128)(2,1)}) custom-call(f32[1024,2048]{1,0:T(8,128)} %get-tuple-element.6.g_ref, bf16[8,2048,256]{2,1,0:T(8,128)(2,1)} %get-tuple-element.7.u_ref), custom_call_target="tpu_custom_call" | custom-call | flops 8589934592 | bytes 33554432 | tf_op jit(solution)/shard_map/pallas_call | solution.py:675
  295.3 0.0 copy-start
  295.3 56.5 %shard_map.52 = bf16[3,512,1024]{2,1,0:T(8,128)(2,1)} custom-call(bf16[2048,1024]{1,0:T(8,128)(2,1)} %get-tuple-element.9.part_ref), custom_call_target="tpu_custom_call" | custom-call | tf_op jit(solution)/shard_map/pallas_call | solution.py:719
  351.8 0.0 copy-done
  351.8 0.1 compare_reduce_fusion
  351.9 4.4 %fusion.1 = f32[512,1024]{1,0:T(8,128)} fusion(bf16[3,512,1024]{2,1,0:T(8,128)(2,1)} %shard_map.52, bf16[2048,1024]{1,0:T(8,128)(2,1)} %get-tuple-element.9.part_ref, s32[]{:T(128)S(6)} %select_n.17, pred[1024]{0:T(1024)(128)(4,1)S(1)} %compare_reduce_fusion), kind=kLoop, calls=%fused_computation.2 | loop fusion | flops 4718592 | bytes 6292484 | tf_op jit(solution)/shard_map/jit(_where)/select_n | solution.py:771
  (1 shorter events, 0.0 us)
Async XLA Ops:
  295.3 56.5 %copy-start = (s32[32]{0:T(128)S(1)}, s32[32]{0:T(128)}, u32[]{:S(2)}) copy-start(s32[32]{0:T(128)} %param.4) | copy-start | bytes 388

commit v4 on v3

--- a/solution.py
+++ b/solution.py
@@ -258,7 +258,26 @@
     return found
 
 
-ORDER = [3, 4, 19, 12, 0, 20, 23, 22, 21, 5, 25, 2, 13, 6, 16, 26, 27, 24, 1, 7, 18, 15, 17, 8, 9, 14, 10, 11]
+def paced(block, s, pieces):
+    if block[0] != block[1]:
+        return s, False
+    unit = pieces // 4
+    late = s - unit
+    if isinstance(s, int):
+        turn = late % 3
+        slow = pieces // 2 + late // 3 * 4 + turn + (turn > 0)
+        return (2 * s, True) if s < unit else (slow, turn == 0)
+    turn = lax.rem(late, 3)
+    slow = pieces // 2 + late // 3 * 4 + turn + jnp.where(turn > 0, 1, 0)
+    return jnp.where(s < unit, 2 * s, slow), (s < unit) | (turn == 0)
+
+
+def span(block, first, last):
+    count = last - first
+    return count // 4 + count // 8 * 3 if block[0] == block[1] else count
+
+
+ORDER = [14, 23, 20, 13, 6, 27, 25, 22, 3, 4, 7, 19, 21, 24, 1, 16, 5, 26, 12, 9, 2, 8, 17, 0, 15, 10, 11, 18]
 
 
 @functools.cache
@@ -273,7 +292,7 @@
         if block == G and final is None:
             due = ready_steps(pieces, hops, pairs)
             final = max(d for key, d in due.items() if key[0] == (1, 0)) + pieces // 4
-        n, at = last - first, {source: final + 1 if block == G else 0}
+        n, at = span(block, first, last), {source: final + 1 if block == G else 0}
         for p, q in route:
             t, used = at[p], busy.setdefault((p, q), [])
             while any(t < e and s < t + n for s, e in used):
@@ -294,7 +313,7 @@
         for chip in (p, q):
             if block[0] != "u" and block not in slots[chip] and block != chip:
                 slots[chip][block] = min(set(range(8)) - set(slots[chip].values()))
-    steps = max([t + last - first + LAG for block, p, q, first, last, t in hops] + [d + pieces // 4 for d in due.values()] + [final + 1])
+    steps = max([t + span(block, first, last) + LAG for block, p, q, first, last, t in hops] + [d + pieces // 4 for d in due.values()] + [final + 1])
     return hops, slots, needs, due, steps, final
 
 
@@ -305,8 +324,10 @@
         ready = {(z, c): [1] * pieces}
         for block, p, q, first, last, t in hops:
             if q == chip:
-                for j in range(first, last):
-                    ready.setdefault(block, [None] * pieces)[j] = t + LAG + j - first
+                for s in range(span(block, first, last)):
+                    j, more = paced(block, s, pieces)
+                    for i in range(1 + more):
+                        ready.setdefault(block, [None] * pieces)[first + j + i] = t + LAG + s
         both = [ready[m, c], ready[m, z]]
         for part in range(4):
             begin = part * (pieces // 4)
@@ -485,21 +506,31 @@
                 for hop in incoming[place]:
                     block, p, q, first, last, t0 = hop
 
-                    @pl.when((t >= t0 + LAG) & (t < t0 + LAG + last - first))
-                    def _():
-                        j = t - (t0 + LAG) + first
+                    def take(j):
                         each(block, j, lambda columns: hop_copy(hop, 0, j, columns).wait_recv())
                         if block[0] == "u":
                             near_copy_u(block[1], j).start()
                         elif block in needs[place]:
                             near_copy(slots[place][block], j).start()
+
+                    @pl.when((t >= t0 + LAG) & (t < t0 + LAG + span(block, first, last)))
+                    def _():
+                        j, more = paced(block, t - (t0 + LAG), pieces)
+                        take(first + j)
+                        if more is not False:
+                            pl.when(more)(functools.partial(take, first + j + 1))
                 for hop, number in outgoing[place]:
                     block, p, q, first, last, t0 = hop
 
-                    @pl.when((t >= t0) & (t < t0 + last - first))
+                    def give(j):
+                        each(block, j, lambda columns: hop_copy(hop, number, j, columns).start())
+
+                    @pl.when((t >= t0) & (t < t0 + span(block, first, last)))
                     def _():
-                        j = t - t0 + first
-                        each(block, j, lambda columns: hop_copy(hop, number, j, columns).start())
+                        j, more = paced(block, t - t0, pieces)
+                        give(first + j)
+                        if more is not False:
+                            pl.when(more)(functools.partial(give, first + j + 1))
 
         def consume(entry, carry):
             pending, into = carry
@@ -656,41 +687,125 @@
     )(factor, coupling)
 
 
-def finish_kernel(g_ref, u_ref, gram_ref, part_ref):
-    gram_ref[...] = g_ref[...]
-    rounded = g_ref[...].astype(u_ref.dtype)
-    narrow = u_ref.shape[2]
+def child_kernel(n_col, g_ref, u_ref, part_ref, other_ref, send, recv, local, whole, held, out):
+    r, c = lax.axis_index("row"), lax.axis_index("col")
+    tile = held.shape[1]
+    count, _, narrow = whole.shape
+    cores = count // n_col
+    tiles = g_ref.shape[0] // tile
+
+    def rows(i):
+        return pl.ds(pl.multiple_of(i * tile, tile), tile)
+
+    def load(i, into):
+        return pltpu.make_async_copy(g_ref.at[rows(i), :], held.at[into], local.at[into])
+
+    def copies(i):
+        found = []
+        for d in range(1, n_col):
+            ct = lax.rem(c + d, n_col)
+            found.append(pltpu.make_async_remote_copy(
+                src_ref=part_ref.at[ct, rows(i), :],
+                dst_ref=other_ref.at[d - 1, rows(i), :],
+                send_sem=send.at[d - 1, i],
+                recv_sem=recv.at[d - 1, i],
+                device_id=(r, ct),
+                device_id_type=MESH,
+            ))
+        return found
+
+    fetch = pltpu.make_async_copy(u_ref, whole, local.at[2])
+    fetch.start()
+    load(0, 0).start()
+    fetch.wait()
 
     def one(i, carry):
-        product = jnp.dot(rounded, u_ref[i], preferred_element_type=jnp.float32)
-        part_ref[pl.ds(pl.multiple_of(i * narrow, narrow), narrow), :] = product.T.astype(part_ref.dtype)
+        into = lax.rem(i, 2)
+        load(i, into).wait()
+
+        @pl.when(i + 1 < tiles)
+        def _():
+            load(i + 1, 1 - into).start()
+        rounded = held[into].astype(whole.dtype)
+        for q in range(count):
+            product = jnp.dot(rounded, whole[q], preferred_element_type=jnp.float32)
+            out[q // cores, :, pl.ds(q % cores * narrow, narrow)] = product.astype(out.dtype)
+        keep = pltpu.make_async_copy(out, part_ref.at[:, rows(i), :], local.at[3])
+        keep.start()
+        keep.wait()
+        for copy in copies(i):
+            copy.start()
         return carry
-    lax.fori_loop(0, u_ref.shape[0], one, 0)
-
-
-def finish(gram, coupling):
+    lax.fori_loop(0, tiles, one, 0)
+
+    def settle(i, carry):
+        for copy in copies(i):
+            copy.wait()
+        return carry
+    lax.fori_loop(0, tiles, settle, 0)
+
+
+def child_parts(gram, coupling, n_col):
     tall, width = gram.shape
     count, depth, narrow = coupling.shape
-    tile = min(256, tall)
+    tile = min(128, tall)
+    wide = count * narrow // n_col
+    dma = pltpu.SemaphoreType.DMA
+    return pl.pallas_call(
+        functools.partial(child_kernel, n_col),
+        out_shape=(
+            jax.ShapeDtypeStruct((n_col, tall, wide), coupling.dtype),
+            jax.ShapeDtypeStruct((n_col - 1, tall, wide), coupling.dtype),
+        ),
+        in_specs=[pl.BlockSpec(memory_space=pl.ANY)] * 2,
+        out_specs=[pl.BlockSpec(memory_space=pl.ANY)] * 2,
+        scratch_shapes=[
+            dma((n_col - 1, tall // tile)),
+            dma((n_col - 1, tall // tile)),
+            dma((4,)),
+            pltpu.VMEM((count, depth, narrow), coupling.dtype),
+            pltpu.VMEM((2, tile, width), gram.dtype),
+            pltpu.VMEM((n_col, tile, wide), coupling.dtype),
+        ],
+        compiler_params=pltpu.CompilerParams(has_side_effects=True, vmem_limit_bytes=63 * 1024 * 1024),
+    )(gram, coupling)
+
+
+def finish_kernel(c_ref, g_ref, own_ref, other_ref, member_ref, gram_ref, child_ref):
+    gram_ref[...] = g_ref[...]
+    total = own_ref[0].astype(jnp.float32)
+    for d in range(other_ref.shape[0]):
+        total = total + other_ref[d].astype(jnp.float32)
+    child_ref[...] = jnp.where(member_ref[...] != 0, -total.T, jnp.float32(0.0))
+
+
+def finish(gram, own, other, member, col_index):
+    tall, width = gram.shape
+    wide = own.shape[2]
+    tile = min(128, tall)
     return pl.pallas_call(
         finish_kernel,
-        grid=(tall // tile,),
+        grid_spec=pltpu.PrefetchScalarGridSpec(
+            num_scalar_prefetch=1,
+            grid=(tall // tile,),
+            in_specs=[
+                pl.BlockSpec((tile, width), lambda i, c: (i, 0)),
+                pl.BlockSpec((1, tile, wide), lambda i, c: (c[0], i, 0)),
+                pl.BlockSpec((other.shape[0], tile, wide), lambda i, c: (0, i, 0)),
+                pl.BlockSpec((1, tile), lambda i, c: (0, i)),
+            ],
+            out_specs=(
+                pl.BlockSpec((tile, width), lambda i, c: (i, 0)),
+                pl.BlockSpec((wide, tile), lambda i, c: (0, i)),
+            ),
+        ),
         out_shape=(
             jax.ShapeDtypeStruct((tall, width), jnp.float32),
-            jax.ShapeDtypeStruct((count * narrow, tall), coupling.dtype),
-        ),
-        in_specs=[
-            pl.BlockSpec((tile, width), lambda i: (i, 0)),
-            pl.BlockSpec((count, depth, narrow), lambda i: (0, 0, 0)),
-        ],
-        out_specs=(
-            pl.BlockSpec((tile, width), lambda i: (i, 0)),
-            pl.BlockSpec((count * narrow, tile), lambda i: (0, i)),
+            jax.ShapeDtypeStruct((wide, tall), jnp.float32),
         ),
         compiler_params=pltpu.CompilerParams(vmem_limit_bytes=63 * 1024 * 1024),
-        cost_estimate=pl.CostEstimate(
-            flops=2 * tall * width * count * narrow, bytes_accessed=tall * width * 16, transcendentals=0),
-    )(gram, coupling)
+        cost_estimate=pl.CostEstimate(flops=0, bytes_accessed=tall * width * 12, transcendentals=0),
+    )(jnp.reshape(col_index, (1,)), gram, own, other, member)
 
 
 def exchange_kernel(n_col, part_ref, out_ref, send, recv):
@@ -756,13 +871,13 @@
     rows_here = factor.shape[0]
     row_index, col_index = lax.axis_index("row"), lax.axis_index("col")
     cores = n_row // n_col
+    global_rows = row_index * rows_here + jnp.arange(rows_here, dtype=jnp.int32)
+    member = jnp.any((global_rows // TILE)[:, None] == sel_tiles[None, :], axis=1)
     if (n_row, n_col) == (8, 4):
         _, pieces, gram = stream(factor, coupling, n_row, n_col)
-        gram, part = finish(gram, pieces)
-    else:
-        gram, part = general(n_row, n_col, factor, coupling)
-    global_rows = row_index * rows_here + jnp.arange(rows_here, dtype=jnp.int32)
-    member = jnp.any((global_rows // TILE)[:, None] == sel_tiles[None, :], axis=1)
+        own, other = child_parts(gram, pieces, n_col)
+        return finish(gram, own, other, member.astype(jnp.int32)[None, :], col_index)
+    gram, part = general(n_row, n_col, factor, coupling)
     depth = part.shape[0] // n_col
     arrived = exchange(part, n_col)
     summed = lax.dynamic_slice_in_dim(part, col_index * depth, depth, 0).astype(jnp.float32)

time: 356 us -> 348 us (0.978)
  Pallas kernels: 351 us -> 347 us
  other arithmetic: 4.49 us -> 0.71 us
    pallas_call x2, Pallas kernels: 79.8 us -> 73.3 us  [the longest x1 62.8 us: child_parts(): pl.pallas_call(functools.partial(child_kernel, n_col), out_shape=(jax.Sha...]
    select_n x1 -> x0, other arithmetic: 4.38 us -> none  [body(): child = jnp.where(member[None, :], -summed, jnp.float32(0.0))]
where the time goes in v4:
time: 348 us
  Pallas kernels  347 us (100%)
    pallas_call x1, Pallas kernels, stream(): pl.pallas_call(functools.partial(stream_kernel, pieces, coupling_pieces),...  273 us
    pallas_call x1, Pallas kernels, child_parts(): pl.pallas_call(functools.partial(child_kernel, n_col), out_shape=(jax.Sha...  62.8 us
    pallas_call x1, Pallas kernels, finish(): pl.pallas_call(finish_kernel, grid_spec=pltpu.PrefetchScalarGridSpec(num_...  10.6 us

profile of v4, /device:TPU:0, one launch (start us, length us, event | category | flops | bytes accessed | tf_op | source)
XLA Modules:
  0.0 348.0 jit_solution(14755864411160535318)
XLA Ops:
  0.6 273.3 %shard_map.50 = (bf16[16384,2048]{1,0:T(8,128)(2,1)}, bf16[8,2048,256]{2,1,0:T(8,128)(2,1)}, f32[1024,2048]{1,0:T(8,128)}) custom-call(bf16[1024,2048]{1,0:T(8,128)(2,1)} %f_ref.1, bf16[2048,256]{1,0:T(8,128)(2,1)} %u_ref.1), custom_call_target="tpu_custom_call" | custom-call | bytes 134217728 | tf_op jit(solution)/shard_map/pallas_call | solution.py:656
  273.9 0.0 copy-start
  274.0 62.8 %shard_map.51 = (bf16[4,1024,512]{2,1,0:T(8,128)(2,1)}, bf16[3,1024,512]{2,1,0:T(8,128)(2,1)}) custom-call(f32[1024,2048]{1,0:T(8,128)} %get-tuple-element.6.g_ref, bf16[8,2048,256]{2,1,0:T(8,128)(2,1)} %get-tuple-element.7.u_ref), custom_call_target="tpu_custom_call" | custom-call | tf_op jit(solution)/shard_map/pallas_call | solution.py:754
  336.8 0.0 copy-done
  336.8 0.1 compare_reduce_fusion
  336.9 0.6 convert_element_type.15
  337.5 10.6 %shard_map.52 = (f32[1024,2048]{1,0:T(8,128)}, f32[512,1024]{1,0:T(8,128)}) custom-call(s32[1]{0:T(128)} %bitcast.c_ref, f32[1024,2048]{1,0:T(8,128)} %get-tuple-element.6.g_ref, bf16[4,1024,512]{2,1,0:T(8,128)(2,1)} %get-tuple-element.8.own_ref, bf16[3,1024,512]{2,1,0:T(8,128)(2,1)} %get-tuple-element.9.other_ref, s32[1,1024]{1,0:T(1,128)} %bitcast.2), custom_call_target="tpu_custom_call" | custom-call | bytes 25165824 | tf_op jit(solution)/shard_map/pallas_call | solution.py:786
  (1 shorter events, 0.0 us)
Async XLA Ops:
  273.9 62.8 %copy-start = (s32[32]{0:T(128)S(1)}, s32[32]{0:T(128)}, u32[]{:S(2)}) copy-start(s32[32]{0:T(128)} %param.4) | copy-start | bytes 388

commit v5 on v4

--- a/solution.py
+++ b/solution.py
@@ -223,7 +223,7 @@
 
 
 def block_flows(pieces):
-    half = pieces // 2
+    half, cut = pieces // 2, 5 * pieces // 8
     found = []
 
     def add(block, source, hops, first=0, last=pieces):
@@ -234,12 +234,14 @@
     add((3, 2), (3, 2), [((3, 2), (2, 2)), ((2, 2), (2, 3)), ((2, 3), (2, 1)), ((2, 2), (2, 0)), ((2, 2), (1, 2)),
                          ((1, 2), (0, 2))])
     add((3, 1), (3, 1), [((3, 1), (2, 1)), ((2, 1), (2, 0)), ((2, 0), (1, 0)), ((1, 0), (1, 1)), ((1, 1), (1, 3)),
-                         ((1, 3), (1, 2))], 0, half)
+                         ((1, 0), (1, 2))], 0, cut)
     add((3, 1), (3, 1), [((3, 1), (2, 1)), ((2, 1), (1, 1)), ((1, 1), (1, 3)), ((1, 3), (1, 2)), ((1, 2), (1, 0))],
-        half, pieces)
+        cut, pieces)
     add((3, 0), (3, 0), [((3, 0), (2, 0)), ((2, 0), (2, 1)), ((2, 1), (2, 3)), ((2, 3), (1, 3)), ((1, 3), (1, 2)),
                          ((1, 2), (1, 0)), ((1, 3), (0, 3)), ((0, 3), (0, 2)), ((0, 2), (0, 0))])
-    add((2, 0), (2, 0), [((2, 0), (1, 0)), ((1, 0), (1, 1)), ((1, 1), (0, 1)), ((0, 1), (0, 0)), ((0, 0), (0, 2))])
+    around = [((1, 0), (1, 1)), ((1, 1), (0, 1)), ((0, 1), (0, 0)), ((0, 0), (0, 2))]
+    add((2, 0), (2, 0), [((2, 0), (1, 0))] + around, 0, 3 * pieces // 4)
+    add((2, 0), (2, 0), [((2, 0), (2, 2)), ((2, 2), (1, 2)), ((1, 2), (1, 0))] + around, 3 * pieces // 4, pieces)
     add((1, 0), (1, 0), [((1, 0), (0, 0))])
     add((2, 1), (2, 1), [((2, 1), (1, 1)), ((1, 1), (1, 0)), ((1, 0), (1, 2))])
     add((1, 1), (1, 1), [((1, 1), (1, 0))])
@@ -277,7 +279,7 @@
     return count // 4 + count // 8 * 3 if block[0] == block[1] else count
 
 
-ORDER = [14, 23, 20, 13, 6, 27, 25, 22, 3, 4, 7, 19, 21, 24, 1, 16, 5, 26, 12, 9, 2, 8, 17, 0, 15, 10, 11, 18]
+ORDER = [6, 24, 14, 15, 3, 9, 25, 13, 7, 17, 5, 4, 8, 26, 1, 2, 20, 10, 19, 0, 28, 16, 18, 21, 12, 11, 23, 22, 27]
 
 
 @functools.cache
@@ -714,10 +716,12 @@
             ))
         return found
 
-    fetch = pltpu.make_async_copy(u_ref, whole, local.at[2])
-    fetch.start()
+    def fetch(q):
+        return pltpu.make_async_copy(u_ref.at[q], whole.at[q], local.at[3 + q])
+
     load(0, 0).start()
-    fetch.wait()
+    for q in range(count):
+        fetch(q).start()
 
     def one(i, carry):
         into = lax.rem(i, 2)
@@ -728,9 +732,10 @@
             load(i + 1, 1 - into).start()
         rounded = held[into].astype(whole.dtype)
         for q in range(count):
+            pl.when(i == 0)(fetch(q).wait)
             product = jnp.dot(rounded, whole[q], preferred_element_type=jnp.float32)
             out[q // cores, :, pl.ds(q % cores * narrow, narrow)] = product.astype(out.dtype)
-        keep = pltpu.make_async_copy(out, part_ref.at[:, rows(i), :], local.at[3])
+        keep = pltpu.make_async_copy(out, part_ref.at[:, rows(i), :], local.at[2])
         keep.start()
         keep.wait()
         for copy in copies(i):
@@ -762,7 +767,7 @@
         scratch_shapes=[
             dma((n_col - 1, tall // tile)),
             dma((n_col - 1, tall // tile)),
-            dma((4,)),
+            dma((3 + count,)),
             pltpu.VMEM((count, depth, narrow), coupling.dtype),
             pltpu.VMEM((2, tile, width), gram.dtype),
             pltpu.VMEM((n_col, tile, wide), coupling.dtype),
@@ -782,7 +787,7 @@
 def finish(gram, own, other, member, col_index):
     tall, width = gram.shape
     wide = own.shape[2]
-    tile = min(128, tall)
+    tile = min(256, tall)
     return pl.pallas_call(
         finish_kernel,
         grid_spec=pltpu.PrefetchScalarGridSpec(

time: 348 us -> 339 us (0.974)
  Pallas kernels: 347 us -> 338 us
    pallas_call x1, Pallas kernels: 273 us -> 262 us  [stream(): pl.pallas_call(functools.partial(stream_kernel, pieces, coupling_pieces),...]
    pallas_call x1, Pallas kernels: 62.8 us -> 66.9 us  [child_parts(): pl.pallas_call(functools.partial(child_kernel, n_col), out_shape=(jax.Sha...]
where the time goes in v5:
time: 339 us
  Pallas kernels  338 us (100%)
    pallas_call x1, Pallas kernels, stream(): pl.pallas_call(functools.partial(stream_kernel, pieces, coupling_pieces),...  262 us
    pallas_call x1, Pallas kernels, child_parts(): pl.pallas_call(functools.partial(child_kernel, n_col), out_shape=(jax.Sha...  66.9 us
    pallas_call x1, Pallas kernels, finish(): pl.pallas_call(finish_kernel, grid_spec=pltpu.PrefetchScalarGridSpec(num_...  8.69 us

profile of v5, /device:TPU:0, one launch (start us, length us, event | category | flops | bytes accessed | tf_op | source)
XLA Modules:
  0.0 338.9 jit_solution(11938027331342318361)
XLA Ops:
  0.6 262.0 %shard_map.50 = (bf16[16384,2048]{1,0:T(8,128)(2,1)}, bf16[8,2048,256]{2,1,0:T(8,128)(2,1)}, f32[1024,2048]{1,0:T(8,128)}) custom-call(bf16[1024,2048]{1,0:T(8,128)(2,1)} %f_ref.1, bf16[2048,256]{1,0:T(8,128)(2,1)} %u_ref.1), custom_call_target="tpu_custom_call" | custom-call | bytes 134217728 | tf_op jit(solution)/shard_map/pallas_call | solution.py:658
  262.6 0.0 copy-start
  262.6 66.9 %shard_map.51 = (bf16[4,1024,512]{2,1,0:T(8,128)(2,1)}, bf16[3,1024,512]{2,1,0:T(8,128)(2,1)}) custom-call(f32[1024,2048]{1,0:T(8,128)} %get-tuple-element.6.g_ref, bf16[8,2048,256]{2,1,0:T(8,128)(2,1)} %get-tuple-element.7.u_ref), custom_call_target="tpu_custom_call" | custom-call | tf_op jit(solution)/shard_map/pallas_call | solution.py:759
  329.5 0.0 copy-done
  329.6 0.1 compare_reduce_fusion
  329.7 0.6 convert_element_type.15
  330.3 8.7 %shard_map.52 = (f32[1024,2048]{1,0:T(8,128)}, f32[512,1024]{1,0:T(8,128)}) custom-call(s32[1]{0:T(128)} %bitcast.c_ref, f32[1024,2048]{1,0:T(8,128)} %get-tuple-element.6.g_ref, bf16[4,1024,512]{2,1,0:T(8,128)(2,1)} %get-tuple-element.8.own_ref, bf16[3,1024,512]{2,1,0:T(8,128)(2,1)} %get-tuple-element.9.other_ref, s32[1,1024]{1,0:T(1,128)} %bitcast.2), custom_call_target="tpu_custom_call" | custom-call | bytes 25165824 | tf_op jit(solution)/shard_map/pallas_call | solution.py:791
  (1 shorter events, 0.0 us)
Async XLA Ops:
  262.6 66.9 %copy-start = (s32[32]{0:T(128)S(1)}, s32[32]{0:T(128)}, u32[]{:S(2)}) copy-start(s32[32]{0:T(128)} %param.4) | copy-start | bytes 388

commit v6 on v5

--- a/solution.py
+++ b/solution.py
@@ -689,8 +689,14 @@
     )(factor, coupling)
 
 
-def child_kernel(n_col, g_ref, u_ref, part_ref, other_ref, send, recv, local, whole, held, out):
+DELAY = 4
+
+
+def child_kernel(n_col, g_ref, u_ref, part_ref, first_ref, second_ref, sum_ref, send, recv, send_sum, recv_sum, local,
+                 whole, held, out, came, mine, both):
     r, c = lax.axis_index("row"), lax.axis_index("col")
+    x, y = lax.rem(c, 2), c // 2
+    beside, above, across = y * 2 + 1 - x, (1 - y) * 2 + x, (1 - y) * 2 + 1 - x
     tile = held.shape[1]
     count, _, narrow = whole.shape
     cores = count // n_col
@@ -699,53 +705,97 @@
     def rows(i):
         return pl.ds(pl.multiple_of(i * tile, tile), tile)
 
+    def pair(i):
+        even = lax.rem(i, 2) == 0
+        return jnp.where(even, beside, above), jnp.where(even, above, beside)
+
+    def remote(src, dst, send_sem, recv_sem, col):
+        return pltpu.make_async_remote_copy(
+            src_ref=src, dst_ref=dst, send_sem=send_sem, recv_sem=recv_sem,
+            device_id=(r, col), device_id_type=MESH,
+        )
+
     def load(i, into):
         return pltpu.make_async_copy(g_ref.at[rows(i), :], held.at[into], local.at[into])
 
-    def copies(i):
-        found = []
-        for d in range(1, n_col):
-            ct = lax.rem(c + d, n_col)
-            found.append(pltpu.make_async_remote_copy(
-                src_ref=part_ref.at[ct, rows(i), :],
-                dst_ref=other_ref.at[d - 1, rows(i), :],
-                send_sem=send.at[d - 1, i],
-                recv_sem=recv.at[d - 1, i],
-                device_id=(r, ct),
-                device_id_type=MESH,
-            ))
-        return found
-
     def fetch(q):
-        return pltpu.make_async_copy(u_ref.at[q], whole.at[q], local.at[3 + q])
+        return pltpu.make_async_copy(u_ref.at[q], whole.at[q], local.at[7 + q])
+
+    def keep(i):
+        return pltpu.make_async_copy(out, part_ref.at[:, rows(i), :], local.at[2])
+
+    def firsts(i):
+        near = pair(i)[0]
+        return [
+            remote(part_ref.at[ct, rows(i), :], first_ref.at[n, rows(i), :], send.at[n, i], recv.at[n, i], near)
+            for n, ct in enumerate((near, across))
+        ]
+
+    def seconds(i):
+        return remote(sum_ref.at[rows(i), :], second_ref.at[rows(i), :], send_sum.at[i], recv_sum.at[i], pair(i)[1])
+
+    def reads(i):
+        return (
+            pltpu.make_async_copy(first_ref.at[1, rows(i), :], came, local.at[3]),
+            pltpu.make_async_copy(part_ref.at[pair(i)[1], rows(i), :], mine, local.at[4]),
+        )
+
+    def store(i):
+        into = lax.rem(i, 2)
+        return pltpu.make_async_copy(both.at[into], sum_ref.at[rows(i), :], local.at[5 + into])
 
     load(0, 0).start()
     for q in range(count):
         fetch(q).start()
 
     def one(i, carry):
-        into = lax.rem(i, 2)
-        load(i, into).wait()
-
-        @pl.when(i + 1 < tiles)
+        @pl.when((i > DELAY) & (i <= tiles + DELAY))
         def _():
-            load(i + 1, 1 - into).start()
-        rounded = held[into].astype(whole.dtype)
-        for q in range(count):
-            pl.when(i == 0)(fetch(q).wait)
-            product = jnp.dot(rounded, whole[q], preferred_element_type=jnp.float32)
-            out[q // cores, :, pl.ds(q % cores * narrow, narrow)] = product.astype(out.dtype)
-        keep = pltpu.make_async_copy(out, part_ref.at[:, rows(i), :], local.at[2])
-        keep.start()
-        keep.wait()
-        for copy in copies(i):
-            copy.start()
+            store(i - DELAY - 1).wait()
+            seconds(i - DELAY - 1).start()
+
+        @pl.when((i >= DELAY) & (i < tiles + DELAY))
+        def _():
+            for copy in firsts(i - DELAY):
+                copy.wait_recv()
+            for copy in reads(i - DELAY):
+                copy.start()
+
+        @pl.when(i < tiles)
+        def _():
+            into = lax.rem(i, 2)
+            load(i, into).wait()
+
+            @pl.when(i + 1 < tiles)
+            def _():
+                load(i + 1, 1 - into).start()
+            rounded = held[into].astype(whole.dtype)
+            for q in range(count):
+                pl.when(i == 0)(fetch(q).wait)
+                product = jnp.dot(rounded, whole[q], preferred_element_type=jnp.float32)
+                out[q // cores, :, pl.ds(q % cores * narrow, narrow)] = product.astype(out.dtype)
+            keep(i).start()
+
+        @pl.when((i >= DELAY) & (i < tiles + DELAY))
+        def _():
+            for copy in reads(i - DELAY):
+                copy.wait()
+            total = came[...].astype(jnp.float32) + mine[...].astype(jnp.float32)
+            both[lax.rem(i - DELAY, 2)] = total.astype(both.dtype)
+            store(i - DELAY).start()
+
+        @pl.when(i < tiles)
+        def _():
+            keep(i).wait()
+            for copy in firsts(i):
+                copy.start()
         return carry
-    lax.fori_loop(0, tiles, one, 0)
+    lax.fori_loop(0, tiles + DELAY + 1, one, 0)
 
     def settle(i, carry):
-        for copy in copies(i):
-            copy.wait()
+        for copy in firsts(i):
+            copy.wait_send()
+        seconds(i).wait()
         return carry
     lax.fori_loop(0, tiles, settle, 0)
 
@@ -755,36 +805,43 @@
     count, depth, narrow = coupling.shape
     tile = min(128, tall)
     wide = count * narrow // n_col
+    tiles = tall // tile
     dma = pltpu.SemaphoreType.DMA
-    return pl.pallas_call(
+    own, first, second, _ = pl.pallas_call(
         functools.partial(child_kernel, n_col),
         out_shape=(
             jax.ShapeDtypeStruct((n_col, tall, wide), coupling.dtype),
-            jax.ShapeDtypeStruct((n_col - 1, tall, wide), coupling.dtype),
+            jax.ShapeDtypeStruct((2, tall, wide), coupling.dtype),
+            jax.ShapeDtypeStruct((tall, wide), coupling.dtype),
+            jax.ShapeDtypeStruct((tall, wide), coupling.dtype),
         ),
         in_specs=[pl.BlockSpec(memory_space=pl.ANY)] * 2,
-        out_specs=[pl.BlockSpec(memory_space=pl.ANY)] * 2,
+        out_specs=[pl.BlockSpec(memory_space=pl.ANY)] * 4,
         scratch_shapes=[
-            dma((n_col - 1, tall // tile)),
-            dma((n_col - 1, tall // tile)),
-            dma((3 + count,)),
+            dma((2, tiles)),
+            dma((2, tiles)),
+            dma((tiles,)),
+            dma((tiles,)),
+            dma((7 + count,)),
             pltpu.VMEM((count, depth, narrow), coupling.dtype),
             pltpu.VMEM((2, tile, width), gram.dtype),
             pltpu.VMEM((n_col, tile, wide), coupling.dtype),
+            pltpu.VMEM((tile, wide), coupling.dtype),
+            pltpu.VMEM((tile, wide), coupling.dtype),
+            pltpu.VMEM((2, tile, wide), coupling.dtype),
         ],
         compiler_params=pltpu.CompilerParams(has_side_effects=True, vmem_limit_bytes=63 * 1024 * 1024),
     )(gram, coupling)
-
-
-def finish_kernel(c_ref, g_ref, own_ref, other_ref, member_ref, gram_ref, child_ref):
+    return own, first, second
+
+
+def finish_kernel(c_ref, g_ref, own_ref, first_ref, second_ref, member_ref, gram_ref, child_ref):
     gram_ref[...] = g_ref[...]
-    total = own_ref[0].astype(jnp.float32)
-    for d in range(other_ref.shape[0]):
-        total = total + other_ref[d].astype(jnp.float32)
+    total = own_ref[0].astype(jnp.float32) + first_ref[0].astype(jnp.float32) + second_ref[...].astype(jnp.float32)
     child_ref[...] = jnp.where(member_ref[...] != 0, -total.T, jnp.float32(0.0))
 
 
-def finish(gram, own, other, member, col_index):
+def finish(gram, own, first, second, member, col_index):
     tall, width = gram.shape
     wide = own.shape[2]
     tile = min(256, tall)
@@ -796,7 +853,8 @@
             in_specs=[
                 pl.BlockSpec((tile, width), lambda i, c: (i, 0)),
                 pl.BlockSpec((1, tile, wide), lambda i, c: (c[0], i, 0)),
-                pl.BlockSpec((other.shape[0], tile, wide), lambda i, c: (0, i, 0)),
+                pl.BlockSpec((1, tile, wide), lambda i, c: (0, i, 0)),
+                pl.BlockSpec((tile, wide), lambda i, c: (i, 0)),
                 pl.BlockSpec((1, tile), lambda i, c: (0, i)),
             ],
             out_specs=(
@@ -810,7 +868,7 @@
         ),
         compiler_params=pltpu.CompilerParams(vmem_limit_bytes=63 * 1024 * 1024),
         cost_estimate=pl.CostEstimate(flops=0, bytes_accessed=tall * width * 12, transcendentals=0),
-    )(jnp.reshape(col_index, (1,)), gram, own, other, member)
+    )(jnp.reshape(col_index, (1,)), gram, own, first, second, member)
 
 
 def exchange_kernel(n_col, part_ref, out_ref, send, recv):
@@ -880,8 +938,8 @@
     member = jnp.any((global_rows // TILE)[:, None] == sel_tiles[None, :], axis=1)
     if (n_row, n_col) == (8, 4):
         _, pieces, gram = stream(factor, coupling, n_row, n_col)
-        own, other = child_parts(gram, pieces, n_col)
-        return finish(gram, own, other, member.astype(jnp.int32)[None, :], col_index)
+        own, first, second = child_parts(gram, pieces, n_col)
+        return finish(gram, own, first, second, member.astype(jnp.int32)[None, :], col_index)
     gram, part = general(n_row, n_col, factor, coupling)
     depth = part.shape[0] // n_col
     arrived = exchange(part, n_col)

time: 339 us -> 336 us (level)
  Pallas kernels: 338 us -> 334 us
where the time goes in v6:
time: 336 us
  Pallas kernels  334 us (99%)
    pallas_call x1, Pallas kernels, stream(): pl.pallas_call(functools.partial(stream_kernel, pieces, coupling_pieces),...  262 us
    pallas_call x1, Pallas kernels, child_parts(): pl.pallas_call(functools.partial(child_kernel, n_col), out_shape=(jax.Sha...  64 us
    pallas_call x1, Pallas kernels, finish(): pl.pallas_call(finish_kernel, grid_spec=pltpu.PrefetchScalarGridSpec(num_...  8.52 us

profile of v6, /device:TPU:0, one launch (start us, length us, event | category | flops | bytes accessed | tf_op | source)
XLA Modules:
  0.0 335.8 jit_solution(11434905468846345336)
XLA Ops:
  0.6 262.0 %shard_map.50 = (bf16[16384,2048]{1,0:T(8,128)(2,1)}, bf16[8,2048,256]{2,1,0:T(8,128)(2,1)}, f32[1024,2048]{1,0:T(8,128)}) custom-call(bf16[1024,2048]{1,0:T(8,128)(2,1)} %f_ref.1, bf16[2048,256]{1,0:T(8,128)(2,1)} %u_ref.1), custom_call_target="tpu_custom_call" | custom-call | bytes 134217728 | tf_op jit(solution)/shard_map/pallas_call | solution.py:658
  262.6 0.0 copy-start
  262.6 64.0 %shard_map.51 = (bf16[4,1024,512]{2,1,0:T(8,128)(2,1)}, bf16[2,1024,512]{2,1,0:T(8,128)(2,1)}, bf16[1024,512]{1,0:T(8,128)(2,1)}, bf16[1024,512]{1,0:T(8,128)(2,1)}) custom-call(f32[1024,2048]{1,0:T(8,128)} %get-tuple-element.7.g_ref, bf16[8,2048,256]{2,1,0:T(8,128)(2,1)} %get-tuple-element.8.u_ref), custom_call_target="tpu_custom_call" | custom-call | tf_op jit(solution)/shard_map/pallas_call | solution.py:810
  326.6 0.0 copy-done
  326.6 0.1 compare_reduce_fusion
  326.7 0.6 convert_element_type.15
  327.3 8.5 %shard_map.52 = (f32[1024,2048]{1,0:T(8,128)}, f32[512,1024]{1,0:T(8,128)}) custom-call(s32[1]{0:T(128)} %bitcast.c_ref, f32[1024,2048]{1,0:T(8,128)} %get-tuple-element.7.g_ref, bf16[4,1024,512]{2,1,0:T(8,128)(2,1)} %get-tuple-element.9.own_ref, bf16[2,1024,512]{2,1,0:T(8,128)(2,1)} %get-tuple-element.10.first_ref, ...), custom_call_target="tpu_custom_call" | custom-call | bytes 25165824 | tf_op jit(solution)/shard_map/pallas_call | solution.py:848
  (1 shorter events, 0.0 us)
Async XLA Ops:
  262.6 64.0 %copy-start = (s32[32]{0:T(128)S(1)}, s32[32]{0:T(128)}, u32[]{:S(2)}) copy-start(s32[32]{0:T(128)} %param.4) | copy-start | bytes 388

commit v7 on v6

--- a/solution.py
+++ b/solution.py
@@ -689,7 +689,7 @@
     )(factor, coupling)
 
 
-DELAY = 4
+DELAY = 3
 
 
 def child_kernel(n_col, g_ref, u_ref, part_ref, first_ref, second_ref, sum_ref, send, recv, send_sum, recv_sum, local,

time: 336 us -> 336 us (level)
  no operation moved by 1% of the time
where the time goes in v7:
time: 336 us
  Pallas kernels  335 us (100%)
    pallas_call x1, Pallas kernels, stream(): pl.pallas_call(functools.partial(stream_kernel, pieces, coupling_pieces),...  262 us
    pallas_call x1, Pallas kernels, child_parts(): pl.pallas_call(functools.partial(child_kernel, n_col), out_shape=(jax.Sha...  64.1 us
    pallas_call x1, Pallas kernels, finish(): pl.pallas_call(finish_kernel, grid_spec=pltpu.PrefetchScalarGridSpec(num_...  8.52 us

profile of v7, /device:TPU:0, one launch (start us, length us, event | category | flops | bytes accessed | tf_op | source)
XLA Modules:
  0.0 336.0 jit_solution(16944817609732542999)
XLA Ops:
  0.6 262.0 %shard_map.50 = (bf16[16384,2048]{1,0:T(8,128)(2,1)}, bf16[8,2048,256]{2,1,0:T(8,128)(2,1)}, f32[1024,2048]{1,0:T(8,128)}) custom-call(bf16[1024,2048]{1,0:T(8,128)(2,1)} %f_ref.1, bf16[2048,256]{1,0:T(8,128)(2,1)} %u_ref.1), custom_call_target="tpu_custom_call" | custom-call | bytes 134217728 | tf_op jit(solution)/shard_map/pallas_call | solution.py:658
  262.6 0.0 copy-start
  262.6 64.1 %shard_map.51 = (bf16[4,1024,512]{2,1,0:T(8,128)(2,1)}, bf16[2,1024,512]{2,1,0:T(8,128)(2,1)}, bf16[1024,512]{1,0:T(8,128)(2,1)}, bf16[1024,512]{1,0:T(8,128)(2,1)}) custom-call(f32[1024,2048]{1,0:T(8,128)} %get-tuple-element.7.g_ref, bf16[8,2048,256]{2,1,0:T(8,128)(2,1)} %get-tuple-element.8.u_ref), custom_call_target="tpu_custom_call" | custom-call | tf_op jit(solution)/shard_map/pallas_call | solution.py:810
  326.7 0.0 copy-done
  326.8 0.1 compare_reduce_fusion
  326.9 0.6 convert_element_type.15
  327.5 8.5 %shard_map.52 = (f32[1024,2048]{1,0:T(8,128)}, f32[512,1024]{1,0:T(8,128)}) custom-call(s32[1]{0:T(128)} %bitcast.c_ref, f32[1024,2048]{1,0:T(8,128)} %get-tuple-element.7.g_ref, bf16[4,1024,512]{2,1,0:T(8,128)(2,1)} %get-tuple-element.9.own_ref, bf16[2,1024,512]{2,1,0:T(8,128)(2,1)} %get-tuple-element.10.first_ref, ...), custom_call_target="tpu_custom_call" | custom-call | bytes 25165824 | tf_op jit(solution)/shard_map/pallas_call | solution.py:848
  (1 shorter events, 0.0 us)
Async XLA Ops:
  262.6 64.1 %copy-start = (s32[32]{0:T(128)S(1)}, s32[32]{0:T(128)}, u32[]{:S(2)}) copy-start(s32[32]{0:T(128)} %param.4) | copy-start | bytes 388
